TPU v7x, 8 devices: a whole 2x2x1 slice. The times are simulated.
8 devices in a mesh: fields: 1 (over z), col: 2 (over y), row: 4 (over x, core).
Axes of the slice: x: 2, y: 2, z: 1, core: 2. Of those that a mesh axis runs over, the one named last changes fastest.
Arguments:
- field_u: bfloat16 [12, 256, 256, 256], P('fields', None, 'row', 'col')
- fac_a: bfloat16 [256, 256], P('fields')
- fac_b: bfloat16 [256, 256], P('fields')
- fac_c: bfloat16 [256, 256], P('fields')
- diag_d: float32 [256, 256, 256], P(('fields', 'row'), 'col')
Outputs:
- output: float32 [12, 256, 256, 256], P('fields', None, 'row', 'col')
All inputs are finite; a program needn't handle non-finite values.
Results may differ from a plain program's by a relative error of at most 0.00205687.
Values are sent between devices in bfloat16 or wider.
A program may use at most 1 GiB of HBM per device.

v0:
```python
import jax
import jax.numpy as jnp
from jax import lax
from jax.experimental import pallas as pl
from jax.experimental.pallas import tpu as pltpu
from jax.sharding import PartitionSpec as P


BF = jnp.bfloat16
F32 = jnp.float32
UNROLL = 2

SLABS = (
    (8, 8, 16, 32,),
    (32, 32,),
    (64,),
    (64,),
    (64,),
    (64,),
    (64,),
    (64,),
    (64,),
    (64,),
    (32, 32,),
    (32, 16, 8, 8,),
)


ORDER = (
    (1, 0, (0, 1, 2, 3)), (2, 0, 1), (2, 0, 0), (3, 0, 1), (2, 0, 2), (3, 0, 0), (1, 1, (0, 1)), (3, 0, 2),
    (2, 0, 3), (1, 8, (0,)), (2, 1, 0), (2, 1, 1), (1, 4, (0,)), (1, 3, (0,)), (3, 0, 3), (1, 5, (0,)),
    (3, 1, 0), (2, 8, 0), (3, 1, 1), (2, 3, 0), (1, 6, (0,)), (2, 4, 0), (3, 8, 0), (1, 11, (0, 1, 2, 3)),
    (1, 10, (0, 1)), (3, 4, 0), (1, 9, (0,)), (2, 6, 0), (2, 5, 0), (1, 2, (0,)), (5, 4, 0), (2, 2, 0),
    (3, 5, 0), (5, 0, 1), (5, 1, 1), (1, 7, (0,)), (3, 3, 0), (3, 2, 0), (2, 7, 0), (5, 5, 0), (5, 3, 0),
    (5, 8, 0), (3, 6, 0), (3, 7, 0), (5, 2, 0), (6, 5, 0), (2, 9, 0), (6, 4, 0), (5, 1, 0), (5, 7, 0),
    (6, 2, 0), (5, 6, 0), (2, 10, 1), (2, 10, 0), (3, 9, 0), (6, 7, 0), (6, 1, 0), (5, 0, 3), (2, 11, 0),
    (3, 10, 1), (2, 11, 2), (5, 0, 0), (6, 3, 0), (3, 10, 0), (5, 0, 2), (6, 6, 0), (5, 9, 0), (3, 11, 0),
    (5, 10, 1), (2, 11, 3), (6, 0, 0), (2, 11, 1), (5, 10, 0), (6, 9, 0), (5, 11, 0), (3, 11, 2), (3, 11, 3),
    (6, 8, 0), (3, 11, 1), (5, 11, 2), (5, 11, 3), (5, 11, 1), (6, 10, 0), (6, 11, 0),
)


def dot(a, b):
    return jnp.dot(a, b, preferred_element_type=F32)


def any_spec():
    return pl.BlockSpec(memory_space=pl.ANY)


def whole(shape):
    return pl.BlockSpec(shape, lambda *g: (0,) * len(shape))


def call(body, token, ins, in_specs, outs, out_specs, grid, flops, alias=None):
    n_in, n_out = len(ins), len(outs)

    def wrapped(token_ref, *refs):
        body(refs[:n_in], refs[n_in:n_in + n_out])

    aliases = {0: n_out}
    aliases.update(alias or {})
    results = pl.pallas_call(
        wrapped,
        grid=grid,
        in_specs=[any_spec()] + list(in_specs),
        out_specs=list(out_specs) + [any_spec()],
        out_shape=list(outs) + [jax.ShapeDtypeStruct(token.shape, token.dtype)],
        input_output_aliases=aliases,
        cost_estimate=pl.CostEstimate(flops=flops, bytes_accessed=1 << 20, transcendentals=0),
        compiler_params=pltpu.CompilerParams(vmem_limit_bytes=67043328),
    )(token, *ins)
    return results[:-1], results[-1]


def stage_one(token, u, a4, b, parts, ny, nz, yb=16, sub=8):
    nx = u.shape[1]
    rows = 4 * sum(s for _, s in parts)

    def body(ins, outs):
        u_ref, a_ref = ins
        a = jnp.concatenate([a_ref[k, o:o + s, :] for o, s in parts for k in range(4)], axis=0)

        def step(t, carry):
            at_y = pl.ds(pl.multiple_of(t * sub, sub), sub)
            flat = u_ref[0, :, at_y, :].reshape(nx, sub * nz)
            h = dot(a, flat).astype(BF).reshape(rows, sub, nz)
            at = 0
            for n, (o, s) in enumerate(parts):
                for k in range(4):
                    outs[4 * n + k][:, at_y, :] = h[at:at + s]
                    at += s
            return carry

        lax.fori_loop(0, yb // sub, step, 0)

    outs = [jax.ShapeDtypeStruct((s, ny, nz), BF) for _, s in parts for _ in range(4)]
    out_specs = [pl.BlockSpec((s, yb, nz), lambda g: (0, g, 0)) for _, s in parts for _ in range(4)]
    return call(body, token, (u, a4), [pl.BlockSpec((1, nx, yb, nz), lambda g: (b, 0, g, 0)), whole(a4.shape)],
                outs, out_specs, (ny // yb,), 2 * rows * nx * ny * nz)


def stage_two(token, pieces, b4, ti=8):
    size, ny, nz = pieces[0].shape
    nj = b4.shape[0] // 2

    def body(ins, outs):
        bm = ins[4][...]

        def step(t, carry):
            i = 2 * t
            y = jnp.concatenate([jnp.concatenate([ins[k][i + e] for k in range(4)], axis=0) for e in range(2)], axis=1)
            h = dot(bm, y).astype(BF)
            for e in range(2):
                for l in range(2):
                    outs[l][i + e] = h[l * nj:(l + 1) * nj, e * nz:(e + 1) * nz]
            return carry

        lax.fori_loop(0, ti // 2, step, 0, unroll=UNROLL)

    out = jax.ShapeDtypeStruct((size, nj, nz), BF)
    return call(body, token, (*pieces, b4), [pl.BlockSpec((ti, ny, nz), lambda g: (g, 0, 0))] * 4 + [whole(b4.shape)],
                [out] * 2, [pl.BlockSpec((ti, nj, nz), lambda g: (g, 0, 0))] * 2, (size // ti,),
                2 * size * 4 * ny * 2 * nj * nz)


def stage_three_four(token, own, got, c_in, c_out, diag, offset, ti=8):
    size, nj, nz = own.shape
    nk = c_out.shape[0]

    def body(ins, outs):
        own_ref, got_ref, ci_ref, co_ref, d_ref = ins
        ci, co = ci_ref[...], co_ref[...]

        def step(t, carry):
            i = 2 * t
            z = jnp.concatenate([jnp.concatenate([own_ref[i + e], got_ref[i + e]], axis=1) for e in range(2)], axis=0)
            h3 = (dot(z, ci) * d_ref[pl.ds(i, 2)].reshape(2 * nj, nk)).astype(BF)
            h4 = dot(h3, co).astype(BF)
            for e in range(2):
                for l in range(2):
                    outs[l][i + e] = h4[e * nj:(e + 1) * nj, l * nz:(l + 1) * nz]
            return carry

        lax.fori_loop(0, ti // 2, step, 0, unroll=UNROLL)

    first = offset // ti
    block = pl.BlockSpec((ti, nj, nz), lambda g: (g, 0, 0))
    out = jax.ShapeDtypeStruct((size, nj, nz), BF)
    return call(body, token, (own, got, c_in, c_out, diag),
                [block] * 2 + [whole(c_in.shape), whole(c_out.shape), pl.BlockSpec((ti, nj, nk), lambda g: (first + g, 0, 0))],
                [out] * 2, [block] * 2, (size // ti,), 4 * size * nj * 2 * nz * nk)


def stage_five(token, own, got, b5, ti=8):
    size, nj, nz = own.shape
    ny = b5.shape[0] // 4

    def body(ins, outs):
        bm = ins[2][...]

        def step(t, carry):
            i = 2 * t
            j = jnp.concatenate([jnp.concatenate([ins[l][i + e] for l in range(2)], axis=0) for e in range(2)], axis=1)
            h = dot(bm, j).astype(BF)
            for e in range(2):
                for k in range(4):
                    outs[k][i + e] = h[k * ny:(k + 1) * ny, e * nz:(e + 1) * nz]
            return carry

        lax.fori_loop(0, ti // 2, step, 0, unroll=UNROLL)

    out = jax.ShapeDtypeStruct((size, ny, nz), BF)
    return call(body, token, (own, got, b5), [pl.BlockSpec((ti, nj, nz), lambda g: (g, 0, 0))] * 2 + [whole(b5.shape)],
                [out] * 4, [pl.BlockSpec((ti, ny, nz), lambda g: (g, 0, 0))] * 4, (size // ti,),
                2 * size * 2 * nj * 4 * ny * nz)


def stage_six(token, pieces, a6, w, b, batch, yb=16, sub=8):
    nx = a6.shape[0]
    _, ny, nz = pieces[0].shape
    n = len(pieces)

    def body(ins, outs):
        def step(t, carry):
            at_y = pl.ds(pl.multiple_of(t * sub, sub), sub)
            x = jnp.concatenate([ref[:, at_y, :] for ref in ins[:n]], axis=0).reshape(a6.shape[1], sub * nz)
            outs[0][0, :, at_y, :] = dot(ins[n][...], x).reshape(nx, sub, nz)
            return carry

        lax.fori_loop(0, yb // sub, step, 0)

    ins = (*pieces, a6)
    in_specs = [pl.BlockSpec((p.shape[0], yb, nz), lambda g: (0, g, 0)) for p in pieces] + [whole(a6.shape)]
    alias = None
    if w is not None:
        ins += (w,)
        in_specs.append(any_spec())
        alias = {len(ins): 0}
    (w,), token = call(body, token, ins, in_specs, [jax.ShapeDtypeStruct((batch, nx, ny, nz), F32)],
                       [pl.BlockSpec((1, nx, yb, nz), lambda g: (b, 0, g, 0))], (ny // yb,),
                       2 * nx * nx * ny * nz, alias)
    return w, token


def solution(mesh):
    spec_field = P("fields", None, "row", "col")
    spec_factor = P("fields", None)
    spec_diag = P(("fields", "row"), "col", None)

    def over_row(outs, m=0):
        got = {}
        for k in (2, 3, 1):
            got[k] = lax.ppermute(outs[k], "row", [(r, r ^ k) for r in range(4)])
            m += 1
        return [outs[0], got[1], got[2], got[3]]

    def over_col(value):
        return lax.ppermute(value, "col", [(0, 1), (1, 0)])

    def local_apply(u, a, bm, cm, diag):
        batch, nx, ny, nz = u.shape
        r, c = lax.axis_index("row"), lax.axis_index("col")
        peers = jnp.bitwise_xor(r, jnp.arange(4))
        sides = jnp.bitwise_xor(c, jnp.arange(2))
        slab = nx // 4
        a4 = jnp.take(a.reshape(4, slab, nx), peers, axis=0)
        a6 = a4.reshape(nx, nx).T
        b4 = jnp.take(bm.reshape(2, nx // 2, 4, nx // 4), sides, axis=0)
        b4 = jnp.take(b4, peers, axis=2).reshape(nx, nx)
        b5 = b4.T
        c_out = jnp.take(cm.reshape(nx, 2, nx // 2), sides, axis=1).reshape(nx, nx)
        c_in = c_out.T
        token = jnp.zeros((8, 128), F32)
        cuts = SLABS
        starts = [[sum(cut[:q]) for q in range(len(cut))] for cut in cuts]
        y_in, z_in, j_in, x_in = {}, {}, {}, {}
        w = None
        for kind, b, q in ORDER:
            if kind == 1:
                parts = [(starts[b][p], cuts[b][p]) for p in q]
                outs, token = stage_one(token, u, a4, b, parts, ny, nz)
                for m, part in enumerate(q):
                    y_in[b, part] = over_row(outs[4 * m:4 * m + 4], 3 * m)
            elif kind == 2:
                (own, other), token = stage_two(token, y_in.pop((b, q)), b4)
                z_in[b, q] = (own, over_col(other))
            elif kind == 3:
                own, got = z_in.pop((b, q))
                (own, other), token = stage_three_four(token, own, got, c_in, c_out, diag, starts[b][q])
                j_in[b, q] = (own, over_col(other))
            elif kind == 5:
                own, got = j_in.pop((b, q))
                outs, token = stage_five(token, own, got, b5)
                x_in[b, q] = over_row(outs)
            else:
                pieces = [x_in[b, p][k] for k in range(4) for p in range(len(cuts[b]))]
                w, token = stage_six(token, pieces, a6, w, b, batch)
        return w

    return jax.shard_map(local_apply, mesh=mesh, in_specs=(spec_field, spec_factor, spec_factor, spec_factor, spec_diag), out_specs=spec_field, check_vma=False)
```

profile of v0, /device:TPU:0, one launch (start us, length us, event | category | flops | bytes accessed | tf_op | source)
XLA Modules:
  0.0 1444.8 jit_solution(7691145589037387573)
XLA Ops:
  101.5 10.4 collective-permute-done.20.refs_3_
  120.8 39.1 %collective-permute-done.46.refs_1_ = bf16[8,128,128]{2,1,0:T(8,128)(2,1)} collective-permute-done((bf16[8,128,128]{2,1,0:T(8,128)(2,1)}, bf16[8,128,128]{2,1,0:T(8,128)(2,1)}, u32[]{:S(2)}, u32[]{:S(2)}) %collective-permute-start.46) | collective-permute-done | bytes 262176 | tf_op jit(solution)/shard_map/ppermute | solution.py:219
  174.6 12.7 collective-permute-done.22.refs_1_
  196.3 17.2 %collective-permute-done.25.refs_3_ = bf16[64,64,128]{2,1,0:T(8,128)(2,1)} collective-permute-done((bf16[64,64,128]{2,1,0:T(8,128)(2,1)}, bf16[64,64,128]{2,1,0:T(8,128)(2,1)}, u32[]{:S(2)}, u32[]{:S(2)}) %collective-permute-start.25) | collective-permute-done | bytes 1048608 | tf_op jit(solution)/shard_map/ppermute | solution.py:214
  235.6 8.4 shard_map.72
  260.5 21.4 %collective-permute-done.28.refs_2_ = bf16[64,64,128]{2,1,0:T(8,128)(2,1)} collective-permute-done((bf16[64,64,128]{2,1,0:T(8,128)(2,1)}, bf16[64,64,128]{2,1,0:T(8,128)(2,1)}, u32[]{:S(2)}, u32[]{:S(2)}) %collective-permute-start.28) | collective-permute-done | bytes 1048608 | tf_op jit(solution)/shard_map/ppermute | solution.py:214
  282.5 20.9 %collective-permute-done.29.refs_3_ = bf16[64,64,128]{2,1,0:T(8,128)(2,1)} collective-permute-done((bf16[64,64,128]{2,1,0:T(8,128)(2,1)}, bf16[64,64,128]{2,1,0:T(8,128)(2,1)}, u32[]{:S(2)}, u32[]{:S(2)}) %collective-permute-start.29) | collective-permute-done | bytes 1048608 | tf_op jit(solution)/shard_map/ppermute | solution.py:214
  304.0 8.4 shard_map.74
  320.5 8.4 shard_map.76
  328.9 30.5 %collective-permute-done.68.refs_1_ = bf16[32,128,128]{2,1,0:T(8,128)(2,1)} collective-permute-done((bf16[32,128,128]{2,1,0:T(8,128)(2,1)}, bf16[32,128,128]{2,1,0:T(8,128)(2,1)}, u32[]{:S(2)}, u32[]{:S(2)}) %collective-permute-start.68) | collective-permute-done | bytes 1048608 | tf_op jit(solution)/shard_map/ppermute | solution.py:219
  363.2 11.7 shard_map.77
  389.1 20.2 %collective-permute-done.37.refs_3_ = bf16[64,64,128]{2,1,0:T(8,128)(2,1)} collective-permute-done((bf16[64,64,128]{2,1,0:T(8,128)(2,1)}, bf16[64,64,128]{2,1,0:T(8,128)(2,1)}, u32[]{:S(2)}, u32[]{:S(2)}) %collective-permute-start.37) | collective-permute-done | bytes 1048608 | tf_op jit(solution)/shard_map/ppermute | solution.py:214
  411.3 40.0 %collective-permute-done.34.refs_1_ = bf16[64,128,128]{2,1,0:T(8,128)(2,1)} collective-permute-done((bf16[64,128,128]{2,1,0:T(8,128)(2,1)}, bf16[64,128,128]{2,1,0:T(8,128)(2,1)}, u32[]{:S(2)}, u32[]{:S(2)}) %collective-permute-start.34) | collective-permute-done | bytes 2097184 | tf_op jit(solution)/shard_map/ppermute | solution.py:219
  468.3 19.8 %collective-permute-done.126.refs_2_ = bf16[16,64,128]{2,1,0:T(8,128)(2,1)} collective-permute-done((bf16[16,64,128]{2,1,0:T(8,128)(2,1)}, bf16[16,64,128]{2,1,0:T(8,128)(2,1)}, u32[]{:S(2)}, u32[]{:S(2)}) %collective-permute-start.126) | collective-permute-done | bytes 262176 | tf_op jit(solution)/shard_map/ppermute | solution.py:214
  495.7 11.7 shard_map.80
  514.6 8.4 shard_map.82
  523.7 8.4 shard_map.83
  543.9 21.9 %collective-permute-done.43.refs_2_ = bf16[64,64,128]{2,1,0:T(8,128)(2,1)} collective-permute-done((bf16[64,64,128]{2,1,0:T(8,128)(2,1)}, bf16[64,64,128]{2,1,0:T(8,128)(2,1)}, u32[]{:S(2)}, u32[]{:S(2)}) %collective-permute-start.43) | collective-permute-done | bytes 1048608 | tf_op jit(solution)/shard_map/ppermute | solution.py:214
  567.3 20.0 %collective-permute-done.44.refs_3_ = bf16[64,64,128]{2,1,0:T(8,128)(2,1)} collective-permute-done((bf16[64,64,128]{2,1,0:T(8,128)(2,1)}, bf16[64,64,128]{2,1,0:T(8,128)(2,1)}, u32[]{:S(2)}, u32[]{:S(2)}) %collective-permute-start.44) | collective-permute-done | bytes 1048608 | tf_op jit(solution)/shard_map/ppermute | solution.py:214
  589.2 8.2 shard_map.85
  597.4 8.3 shard_map.86
  605.7 20.1 %collective-permute-done.45.refs_1_ = bf16[64,128,128]{2,1,0:T(8,128)(2,1)} collective-permute-done((bf16[64,128,128]{2,1,0:T(8,128)(2,1)}, bf16[64,128,128]{2,1,0:T(8,128)(2,1)}, u32[]{:S(2)}, u32[]{:S(2)}) %collective-permute-start.45) | collective-permute-done | bytes 2097184 | tf_op jit(solution)/shard_map/ppermute | solution.py:219
  626.4 11.7 shard_map.87
  652.5 18.3 %collective-permute-done.55.refs_1_ = bf16[64,128,128]{2,1,0:T(8,128)(2,1)} collective-permute-done((bf16[64,128,128]{2,1,0:T(8,128)(2,1)}, bf16[64,128,128]{2,1,0:T(8,128)(2,1)}, u32[]{:S(2)}, u32[]{:S(2)}) %collective-permute-start.55) | collective-permute-done | bytes 2097184 | tf_op jit(solution)/shard_map/ppermute | solution.py:219
  671.8 44.0 %collective-permute-done.56.refs_1_ = bf16[64,128,128]{2,1,0:T(8,128)(2,1)} collective-permute-done((bf16[64,128,128]{2,1,0:T(8,128)(2,1)}, bf16[64,128,128]{2,1,0:T(8,128)(2,1)}, u32[]{:S(2)}, u32[]{:S(2)}) %collective-permute-start.56) | collective-permute-done | bytes 2097184 | tf_op jit(solution)/shard_map/ppermute | solution.py:219
  717.6 26.4 %collective-permute-done.122.refs_13_ = bf16[8,64,128]{2,1,0:T(8,128)(2,1)} collective-permute-done((bf16[8,64,128]{2,1,0:T(8,128)(2,1)}, bf16[8,64,128]{2,1,0:T(8,128)(2,1)}, u32[]{:S(2)}, u32[]{:S(2)}) %collective-permute-start.122) | collective-permute-done | bytes 131104 | tf_op jit(solution)/shard_map/ppermute | solution.py:214
  746.7 11.7 shard_map.91
  759.9 9.1 collective-permute-done.52.refs_3_
  771.2 11.7 shard_map.92
  782.9 8.3 shard_map.93
  793.7 11.9 collective-permute-done.53.refs_1_
  806.2 8.1 shard_map.94
  818.2 32.4 %collective-permute-done.54.refs_1_ = bf16[64,128,128]{2,1,0:T(8,128)(2,1)} collective-permute-done((bf16[64,128,128]{2,1,0:T(8,128)(2,1)}, bf16[64,128,128]{2,1,0:T(8,128)(2,1)}, u32[]{:S(2)}, u32[]{:S(2)}) %collective-permute-start.54) | collective-permute-done | bytes 2097184 | tf_op jit(solution)/shard_map/ppermute | solution.py:219
  851.5 8.2 shard_map.95
  859.7 8.1 shard_map.96
  867.9 11.7 shard_map.97
  879.6 15.9 %collective-permute-done.57.refs_1_ = bf16[64,128,128]{2,1,0:T(8,128)(2,1)} collective-permute-done((bf16[64,128,128]{2,1,0:T(8,128)(2,1)}, bf16[64,128,128]{2,1,0:T(8,128)(2,1)}, u32[]{:S(2)}, u32[]{:S(2)}) %collective-permute-start.57) | collective-permute-done | bytes 2097184 | tf_op jit(solution)/shard_map/ppermute | solution.py:219
  896.0 11.7 shard_map.98
  909.7 30.7 %collective-permute-done.58.refs_1_ = bf16[64,128,128]{2,1,0:T(8,128)(2,1)} collective-permute-done((bf16[64,128,128]{2,1,0:T(8,128)(2,1)}, bf16[64,128,128]{2,1,0:T(8,128)(2,1)}, u32[]{:S(2)}, u32[]{:S(2)}) %collective-permute-start.58) | collective-permute-done | bytes 2097184 | tf_op jit(solution)/shard_map/ppermute | solution.py:219
  941.4 8.1 shard_map.99
  949.5 7.5 shard_map.100
  957.0 8.4 shard_map.101
  967.0 18.3 %collective-permute-done.73.refs_1_ = bf16[64,128,128]{2,1,0:T(8,128)(2,1)} collective-permute-done((bf16[64,128,128]{2,1,0:T(8,128)(2,1)}, bf16[64,128,128]{2,1,0:T(8,128)(2,1)}, u32[]{:S(2)}, u32[]{:S(2)}) %collective-permute-start.73) | collective-permute-done | bytes 2097184 | tf_op jit(solution)/shard_map/ppermute | solution.py:219
  985.4 44.9 %collective-permute-done.69.refs_1_ = bf16[64,128,128]{2,1,0:T(8,128)(2,1)} collective-permute-done((bf16[64,128,128]{2,1,0:T(8,128)(2,1)}, bf16[64,128,128]{2,1,0:T(8,128)(2,1)}, u32[]{:S(2)}, u32[]{:S(2)}) %collective-permute-start.69) | collective-permute-done | bytes 2097184 | tf_op jit(solution)/shard_map/ppermute | solution.py:219
  1030.3 7.5 shard_map.102
  1042.5 8.2 shard_map.104
  1060.7 8.1 shard_map.106
  1082.5 11.7 shard_map.109
  1094.2 10.7 collective-permute-done.102.refs_1_
  1105.5 21.9 %collective-permute-done.94.refs_1_ = bf16[32,128,128]{2,1,0:T(8,128)(2,1)} collective-permute-done((bf16[32,128,128]{2,1,0:T(8,128)(2,1)}, bf16[32,128,128]{2,1,0:T(8,128)(2,1)}, u32[]{:S(2)}, u32[]{:S(2)}) %collective-permute-start.94) | collective-permute-done | bytes 1048608 | tf_op jit(solution)/shard_map/ppermute | solution.py:219
  1137.8 7.8 shard_map.111
  1166.3 7.5 shard_map.117
  1184.6 12.6 collective-permute-done.106.refs_3_
  1200.2 15.0 %collective-permute-done.121.refs_12_ = bf16[8,64,128]{2,1,0:T(8,128)(2,1)} collective-permute-done((bf16[8,64,128]{2,1,0:T(8,128)(2,1)}, bf16[8,64,128]{2,1,0:T(8,128)(2,1)}, u32[]{:S(2)}, u32[]{:S(2)}) %collective-permute-start.121) | collective-permute-done | bytes 131104 | tf_op jit(solution)/shard_map/ppermute | solution.py:214
  1226.2 7.5 shard_map.120
  1233.7 8.2 shard_map.121
  1256.2 13.4 collective-permute-done.109.refs_1_
  1277.2 14.9 %collective-permute-done.128.refs_1_ = bf16[32,128,128]{2,1,0:T(8,128)(2,1)} collective-permute-done((bf16[32,128,128]{2,1,0:T(8,128)(2,1)}, bf16[32,128,128]{2,1,0:T(8,128)(2,1)}, u32[]{:S(2)}, u32[]{:S(2)}) %collective-permute-start.128) | collective-permute-done | bytes 1048608 | tf_op jit(solution)/shard_map/ppermute | solution.py:219
  1292.6 26.4 %collective-permute-done.134.refs_1_ = bf16[8,128,128]{2,1,0:T(8,128)(2,1)} collective-permute-done((bf16[8,128,128]{2,1,0:T(8,128)(2,1)}, bf16[8,128,128]{2,1,0:T(8,128)(2,1)}, u32[]{:S(2)}, u32[]{:S(2)}) %collective-permute-start.134) | collective-permute-done | bytes 262176 | tf_op jit(solution)/shard_map/ppermute | solution.py:219
  1319.0 7.9 shard_map.125
  1359.0 8.2 collective-permute-done.146.refs_6_
  1400.6 20.6 %collective-permute-done.154.refs_10_ = bf16[8,64,128]{2,1,0:T(8,128)(2,1)} collective-permute-done((bf16[8,64,128]{2,1,0:T(8,128)(2,1)}, bf16[8,64,128]{2,1,0:T(8,128)(2,1)}, u32[]{:S(2)}, u32[]{:S(2)}) %collective-permute-start.154) | collective-permute-done | bytes 131104 | tf_op jit(solution)/shard_map/ppermute | solution.py:214
  1424.4 7.8 shard_map.137
  1436.9 7.7 shard_map.138
  (381 shorter events, 467.6 us)
Async XLA Ops:
  85.0 88.8 %collective-permute-start.21 = (bf16[32,128,128]{2,1,0:T(8,128)(2,1)}, bf16[32,128,128]{2,1,0:T(8,128)(2,1)}, u32[]{:S(2)}, u32[]{:S(2)}) collective-permute-start(bf16[32,128,128]{2,1,0:T(8,128)(2,1)} %get-tuple-element.385), channel_id=1, source_target_pairs={{0,4},{4,0},{1,5},{5,1},{2,6},{6,2},{3,7},{7,3}} | collective-permute-start | bytes 3145736 | tf_op jit(solution)/shard_map/ppermute | solution.py:219
  116.8 57.5 %collective-permute-start.26 = (bf16[32,128,128]{2,1,0:T(8,128)(2,1)}, bf16[32,128,128]{2,1,0:T(8,128)(2,1)}, u32[]{:S(2)}, u32[]{:S(2)}) collective-permute-start(bf16[32,128,128]{2,1,0:T(8,128)(2,1)} %get-tuple-element.397), channel_id=1, source_target_pairs={{0,4},{4,0},{1,5},{5,1},{2,6},{6,2},{3,7},{7,3}} | collective-permute-start | bytes 3145736 | tf_op jit(solution)/shard_map/ppermute | solution.py:219
  117.5 48.1 %collective-permute-start.103 = (bf16[16,128,128]{2,1,0:T(8,128)(2,1)}, bf16[16,128,128]{2,1,0:T(8,128)(2,1)}, u32[]{:S(2)}, u32[]{:S(2)}) collective-permute-start(bf16[16,128,128]{2,1,0:T(8,128)(2,1)} %get-tuple-element.566), channel_id=1, source_target_pairs={{0,4},{4,0},{1,5},{5,1},{2,6},{6,2},{3,7},{7,3}} | collective-permute-start | bytes 1572872 | tf_op jit(solution)/shard_map/ppermute | solution.py:219
  119.5 46.1 %collective-permute-start.98 = (bf16[8,128,128]{2,1,0:T(8,128)(2,1)}, bf16[8,128,128]{2,1,0:T(8,128)(2,1)}, u32[]{:S(2)}, u32[]{:S(2)}) collective-permute-start(bf16[8,128,128]{2,1,0:T(8,128)(2,1)} %get-tuple-element.554), channel_id=1, source_target_pairs={{0,4},{4,0},{1,5},{5,1},{2,6},{6,2},{3,7},{7,3}} | collective-permute-start | bytes 786440 | tf_op jit(solution)/shard_map/ppermute | solution.py:219
  187.3 56.6 %collective-permute-start.31 = (bf16[64,64,128]{2,1,0:T(8,128)(2,1)}, bf16[64,64,128]{2,1,0:T(8,128)(2,1)}, u32[]{:S(2)}, u32[]{:S(2)}) collective-permute-start(bf16[64,64,128]{2,1,0:T(8,128)(2,1)} %get-tuple-element.407), channel_id=1, source_target_pairs={{0,2},{1,3},{2,0},{3,1},{4,6},{5,7},{6,4},{7,5}} | collective-permute-start | bytes 3145736 | tf_op jit(solution)/shard_map/ppermute | solution.py:214
  188.8 69.6 %collective-permute-start.32 = (bf16[64,64,128]{2,1,0:T(8,128)(2,1)}, bf16[64,64,128]{2,1,0:T(8,128)(2,1)}, u32[]{:S(2)}, u32[]{:S(2)}) collective-permute-start(bf16[64,64,128]{2,1,0:T(8,128)(2,1)} %get-tuple-element.408), channel_id=1, source_target_pairs={{0,3},{1,2},{2,1},{3,0},{4,7},{5,6},{6,5},{7,4}} | collective-permute-start | bytes 3145736 | tf_op jit(solution)/shard_map/ppermute | solution.py:214
  195.7 63.5 %collective-permute-start.27 = (bf16[64,64,128]{2,1,0:T(8,128)(2,1)}, bf16[64,64,128]{2,1,0:T(8,128)(2,1)}, u32[]{:S(2)}, u32[]{:S(2)}) collective-permute-start(bf16[64,64,128]{2,1,0:T(8,128)(2,1)} %get-tuple-element.400), channel_id=1, source_target_pairs={{0,1},{1,0},{2,3},{3,2},{4,5},{5,4},{6,7},{7,6}} | collective-permute-start | bytes 3145736 | tf_op jit(solution)/shard_map/ppermute | solution.py:214
  213.5 68.3 %collective-permute-start.28 = (bf16[64,64,128]{2,1,0:T(8,128)(2,1)}, bf16[64,64,128]{2,1,0:T(8,128)(2,1)}, u32[]{:S(2)}, u32[]{:S(2)}) collective-permute-start(bf16[64,64,128]{2,1,0:T(8,128)(2,1)} %get-tuple-element.401), channel_id=1, source_target_pairs={{0,2},{1,3},{2,0},{3,1},{4,6},{5,7},{6,4},{7,5}} | collective-permute-start | bytes 3145736 | tf_op jit(solution)/shard_map/ppermute | solution.py:214
  214.9 88.5 %collective-permute-start.29 = (bf16[64,64,128]{2,1,0:T(8,128)(2,1)}, bf16[64,64,128]{2,1,0:T(8,128)(2,1)}, u32[]{:S(2)}, u32[]{:S(2)}) collective-permute-start(bf16[64,64,128]{2,1,0:T(8,128)(2,1)} %get-tuple-element.402), channel_id=1, source_target_pairs={{0,3},{1,2},{2,1},{3,0},{4,7},{5,6},{6,5},{7,4}} | collective-permute-start | bytes 3145736 | tf_op jit(solution)/shard_map/ppermute | solution.py:214
  244.0 68.4 %collective-permute-start.90 = (bf16[32,128,128]{2,1,0:T(8,128)(2,1)}, bf16[32,128,128]{2,1,0:T(8,128)(2,1)}, u32[]{:S(2)}, u32[]{:S(2)}) collective-permute-start(bf16[32,128,128]{2,1,0:T(8,128)(2,1)} %get-tuple-element.538), channel_id=1, source_target_pairs={{0,4},{4,0},{1,5},{5,1},{2,6},{6,2},{3,7},{7,3}} | collective-permute-start | bytes 3145736 | tf_op jit(solution)/shard_map/ppermute | solution.py:219
  258.5 62.0 %collective-permute-start.47 = (bf16[32,128,128]{2,1,0:T(8,128)(2,1)}, bf16[32,128,128]{2,1,0:T(8,128)(2,1)}, u32[]{:S(2)}, u32[]{:S(2)}) collective-permute-start(bf16[32,128,128]{2,1,0:T(8,128)(2,1)} %get-tuple-element.445), channel_id=1, source_target_pairs={{0,4},{4,0},{1,5},{5,1},{2,6},{6,2},{3,7},{7,3}} | collective-permute-start | bytes 3145736 | tf_op jit(solution)/shard_map/ppermute | solution.py:219
  259.1 103.6 %collective-permute-start.33 = (bf16[64,128,128]{2,1,0:T(8,128)(2,1)}, bf16[64,128,128]{2,1,0:T(8,128)(2,1)}, u32[]{:S(2)}, u32[]{:S(2)}) collective-permute-start(bf16[64,128,128]{2,1,0:T(8,128)(2,1)} %get-tuple-element.411), channel_id=1, source_target_pairs={{0,4},{4,0},{1,5},{5,1},{2,6},{6,2},{3,7},{7,3}} | collective-permute-start | bytes 6291464 | tf_op jit(solution)/shard_map/ppermute | solution.py:219
  281.8 77.5 %collective-permute-start.68 = (bf16[32,128,128]{2,1,0:T(8,128)(2,1)}, bf16[32,128,128]{2,1,0:T(8,128)(2,1)}, u32[]{:S(2)}, u32[]{:S(2)}) collective-permute-start(bf16[32,128,128]{2,1,0:T(8,128)(2,1)} %get-tuple-element.494), channel_id=1, source_target_pairs={{0,4},{4,0},{1,5},{5,1},{2,6},{6,2},{3,7},{7,3}} | collective-permute-start | bytes 3145736 | tf_op jit(solution)/shard_map/ppermute | solution.py:219
  303.4 56.6 %collective-permute-start.38 = (bf16[64,64,128]{2,1,0:T(8,128)(2,1)}, bf16[64,64,128]{2,1,0:T(8,128)(2,1)}, u32[]{:S(2)}, u32[]{:S(2)}) collective-permute-start(bf16[64,64,128]{2,1,0:T(8,128)(2,1)} %get-tuple-element.425), channel_id=1, source_target_pairs={{0,1},{1,0},{2,3},{3,2},{4,5},{5,4},{6,7},{7,6}} | collective-permute-start | bytes 3145736 | tf_op jit(solution)/shard_map/ppermute | solution.py:214
  312.4 49.0 %collective-permute-start.39 = (bf16[64,64,128]{2,1,0:T(8,128)(2,1)}, bf16[64,64,128]{2,1,0:T(8,128)(2,1)}, u32[]{:S(2)}, u32[]{:S(2)}) collective-permute-start(bf16[64,64,128]{2,1,0:T(8,128)(2,1)} %get-tuple-element.426), channel_id=1, source_target_pairs={{0,2},{1,3},{2,0},{3,1},{4,6},{5,7},{6,4},{7,5}} | collective-permute-start | bytes 3145736 | tf_op jit(solution)/shard_map/ppermute | solution.py:214
  359.3 51.9 %collective-permute-start.48 = (bf16[64,128,128]{2,1,0:T(8,128)(2,1)}, bf16[64,128,128]{2,1,0:T(8,128)(2,1)}, u32[]{:S(2)}, u32[]{:S(2)}) collective-permute-start(bf16[64,128,128]{2,1,0:T(8,128)(2,1)} %get-tuple-element.449), channel_id=1, source_target_pairs={{0,4},{4,0},{1,5},{5,1},{2,6},{6,2},{3,7},{7,3}} | collective-permute-start | bytes 6291464 | tf_op jit(solution)/shard_map/ppermute | solution.py:219
  360.0 91.3 %collective-permute-start.34 = (bf16[64,128,128]{2,1,0:T(8,128)(2,1)}, bf16[64,128,128]{2,1,0:T(8,128)(2,1)}, u32[]{:S(2)}, u32[]{:S(2)}) collective-permute-start(bf16[64,128,128]{2,1,0:T(8,128)(2,1)} %get-tuple-element.416), channel_id=1, source_target_pairs={{0,4},{4,0},{1,5},{5,1},{2,6},{6,2},{3,7},{7,3}} | collective-permute-start | bytes 6291464 | tf_op jit(solution)/shard_map/ppermute | solution.py:219
  362.7 46.5 %collective-permute-start.37 = (bf16[64,64,128]{2,1,0:T(8,128)(2,1)}, bf16[64,64,128]{2,1,0:T(8,128)(2,1)}, u32[]{:S(2)}, u32[]{:S(2)}) collective-permute-start(bf16[64,64,128]{2,1,0:T(8,128)(2,1)} %get-tuple-element.422), channel_id=1, source_target_pairs={{0,3},{1,2},{2,1},{3,0},{4,7},{5,6},{6,5},{7,4}} | collective-permute-start | bytes 3145736 | tf_op jit(solution)/shard_map/ppermute | solution.py:214
  381.8 70.9 %collective-permute-start.95 = (bf16[8,64,128]{2,1,0:T(8,128)(2,1)}, bf16[8,64,128]{2,1,0:T(8,128)(2,1)}, u32[]{:S(2)}, u32[]{:S(2)}) collective-permute-start(bf16[8,64,128]{2,1,0:T(8,128)(2,1)} %get-tuple-element.549), channel_id=1, source_target_pairs={{0,1},{1,0},{2,3},{3,2},{4,5},{5,4},{6,7},{7,6}} | collective-permute-start | bytes 393224 | tf_op jit(solution)/shard_map/ppermute | solution.py:214
  387.7 64.9 %collective-permute-start.96 = (bf16[8,64,128]{2,1,0:T(8,128)(2,1)}, bf16[8,64,128]{2,1,0:T(8,128)(2,1)}, u32[]{:S(2)}, u32[]{:S(2)}) collective-permute-start(bf16[8,64,128]{2,1,0:T(8,128)(2,1)} %get-tuple-element.550), channel_id=1, source_target_pairs={{0,2},{1,3},{2,0},{3,1},{4,6},{5,7},{6,4},{7,5}} | collective-permute-start | bytes 393224 | tf_op jit(solution)/shard_map/ppermute | solution.py:214
  494.3 45.1 %collective-permute-start.77 = (bf16[32,64,128]{2,1,0:T(8,128)(2,1)}, bf16[32,64,128]{2,1,0:T(8,128)(2,1)}, u32[]{:S(2)}, u32[]{:S(2)}) collective-permute-start(bf16[32,64,128]{2,1,0:T(8,128)(2,1)} %get-tuple-element.514), channel_id=1, source_target_pairs={{0,1},{1,0},{2,3},{3,2},{4,5},{5,4},{6,7},{7,6}} | collective-permute-start | bytes 1572872 | tf_op jit(solution)/shard_map/ppermute | solution.py:214
  532.1 56.2 %collective-permute-start.41 = (bf16[64,128,128]{2,1,0:T(8,128)(2,1)}, bf16[64,128,128]{2,1,0:T(8,128)(2,1)}, u32[]{:S(2)}, u32[]{:S(2)}) collective-permute-start(bf16[64,128,128]{2,1,0:T(8,128)(2,1)} %get-tuple-element.431), channel_id=1, source_target_pairs={{0,4},{4,0},{1,5},{5,1},{2,6},{6,2},{3,7},{7,3}} | collective-permute-start | bytes 6291464 | tf_op jit(solution)/shard_map/ppermute | solution.py:219
  540.4 85.4 %collective-permute-start.45 = (bf16[64,128,128]{2,1,0:T(8,128)(2,1)}, bf16[64,128,128]{2,1,0:T(8,128)(2,1)}, u32[]{:S(2)}, u32[]{:S(2)}) collective-permute-start(bf16[64,128,128]{2,1,0:T(8,128)(2,1)} %get-tuple-element.439), channel_id=1, source_target_pairs={{0,4},{4,0},{1,5},{5,1},{2,6},{6,2},{3,7},{7,3}} | collective-permute-start | bytes 6291464 | tf_op jit(solution)/shard_map/ppermute | solution.py:219
  541.9 45.3 %collective-permute-start.44 = (bf16[64,64,128]{2,1,0:T(8,128)(2,1)}, bf16[64,64,128]{2,1,0:T(8,128)(2,1)}, u32[]{:S(2)}, u32[]{:S(2)}) collective-permute-start(bf16[64,64,128]{2,1,0:T(8,128)(2,1)} %get-tuple-element.436), channel_id=1, source_target_pairs={{0,3},{1,2},{2,1},{3,0},{4,7},{5,6},{6,5},{7,4}} | collective-permute-start | bytes 3145736 | tf_op jit(solution)/shard_map/ppermute | solution.py:214
  542.5 128.3 %collective-permute-start.55 = (bf16[64,128,128]{2,1,0:T(8,128)(2,1)}, bf16[64,128,128]{2,1,0:T(8,128)(2,1)}, u32[]{:S(2)}, u32[]{:S(2)}) collective-permute-start(bf16[64,128,128]{2,1,0:T(8,128)(2,1)} %get-tuple-element.466), channel_id=1, source_target_pairs={{0,4},{4,0},{1,5},{5,1},{2,6},{6,2},{3,7},{7,3}} | collective-permute-start | bytes 6291464 | tf_op jit(solution)/shard_map/ppermute | solution.py:219
  565.8 149.9 %collective-permute-start.56 = (bf16[64,128,128]{2,1,0:T(8,128)(2,1)}, bf16[64,128,128]{2,1,0:T(8,128)(2,1)}, u32[]{:S(2)}, u32[]{:S(2)}) collective-permute-start(bf16[64,128,128]{2,1,0:T(8,128)(2,1)} %get-tuple-element.469), channel_id=1, source_target_pairs={{0,4},{4,0},{1,5},{5,1},{2,6},{6,2},{3,7},{7,3}} | collective-permute-start | bytes 6291464 | tf_op jit(solution)/shard_map/ppermute | solution.py:219
  587.3 64.7 %collective-permute-start.63 = (bf16[64,64,128]{2,1,0:T(8,128)(2,1)}, bf16[64,64,128]{2,1,0:T(8,128)(2,1)}, u32[]{:S(2)}, u32[]{:S(2)}) collective-permute-start(bf16[64,64,128]{2,1,0:T(8,128)(2,1)} %get-tuple-element.484), channel_id=1, source_target_pairs={{0,2},{1,3},{2,0},{3,1},{4,6},{5,7},{6,4},{7,5}} | collective-permute-start | bytes 3145736 | tf_op jit(solution)/shard_map/ppermute | solution.py:214
  588.2 63.7 %collective-permute-start.64 = (bf16[64,64,128]{2,1,0:T(8,128)(2,1)}, bf16[64,64,128]{2,1,0:T(8,128)(2,1)}, u32[]{:S(2)}, u32[]{:S(2)}) collective-permute-start(bf16[64,64,128]{2,1,0:T(8,128)(2,1)} %get-tuple-element.485), channel_id=1, source_target_pairs={{0,3},{1,2},{2,1},{3,0},{4,7},{5,6},{6,5},{7,4}} | collective-permute-start | bytes 3145736 | tf_op jit(solution)/shard_map/ppermute | solution.py:214
  625.8 144.8 %collective-permute-start.49 = (bf16[64,128,128]{2,1,0:T(8,128)(2,1)}, bf16[64,128,128]{2,1,0:T(8,128)(2,1)}, u32[]{:S(2)}, u32[]{:S(2)}) collective-permute-start(bf16[64,128,128]{2,1,0:T(8,128)(2,1)} %get-tuple-element.452), channel_id=1, source_target_pairs={{0,4},{4,0},{1,5},{5,1},{2,6},{6,2},{3,7},{7,3}} | collective-permute-start | bytes 6291464 | tf_op jit(solution)/shard_map/ppermute | solution.py:219
  651.9 93.7 %collective-permute-start.50 = (bf16[64,64,128]{2,1,0:T(8,128)(2,1)}, bf16[64,64,128]{2,1,0:T(8,128)(2,1)}, u32[]{:S(2)}, u32[]{:S(2)}) collective-permute-start(bf16[64,64,128]{2,1,0:T(8,128)(2,1)} %get-tuple-element.455), channel_id=1, source_target_pairs={{0,1},{1,0},{2,3},{3,2},{4,5},{5,4},{6,7},{7,6}} | collective-permute-start | bytes 3145736 | tf_op jit(solution)/shard_map/ppermute | solution.py:214
  652.0 63.8 %collective-permute-start.114 = (bf16[8,64,128]{2,1,0:T(8,128)(2,1)}, bf16[8,64,128]{2,1,0:T(8,128)(2,1)}, u32[]{:S(2)}, u32[]{:S(2)}) collective-permute-start(bf16[8,64,128]{2,1,0:T(8,128)(2,1)} %get-tuple-element.593), channel_id=1, source_target_pairs={{0,1},{1,0},{2,3},{3,2},{4,5},{5,4},{6,7},{7,6}} | collective-permute-start | bytes 393224 | tf_op jit(solution)/shard_map/ppermute | solution.py:214
  670.8 45.9 %collective-permute-start.118 = (bf16[8,64,128]{2,1,0:T(8,128)(2,1)}, bf16[8,64,128]{2,1,0:T(8,128)(2,1)}, u32[]{:S(2)}, u32[]{:S(2)}) collective-permute-start(bf16[8,64,128]{2,1,0:T(8,128)(2,1)} %get-tuple-element.597), channel_id=1, source_target_pairs={{0,2},{1,3},{2,0},{3,1},{4,6},{5,7},{6,4},{7,5}} | collective-permute-start | bytes 393224 | tf_op jit(solution)/shard_map/ppermute | solution.py:214
  745.1 60.5 %collective-permute-start.53 = (bf16[64,128,128]{2,1,0:T(8,128)(2,1)}, bf16[64,128,128]{2,1,0:T(8,128)(2,1)}, u32[]{:S(2)}, u32[]{:S(2)}) collective-permute-start(bf16[64,128,128]{2,1,0:T(8,128)(2,1)} %get-tuple-element.460), channel_id=1, source_target_pairs={{0,4},{4,0},{1,5},{5,1},{2,6},{6,2},{3,7},{7,3}} | collective-permute-start | bytes 6291464 | tf_op jit(solution)/shard_map/ppermute | solution.py:219
  745.7 45.6 %collective-permute-start.87 = (bf16[32,64,128]{2,1,0:T(8,128)(2,1)}, bf16[32,64,128]{2,1,0:T(8,128)(2,1)}, u32[]{:S(2)}, u32[]{:S(2)}) collective-permute-start(bf16[32,64,128]{2,1,0:T(8,128)(2,1)} %get-tuple-element.532), channel_id=1, source_target_pairs={{0,2},{1,3},{2,0},{3,1},{4,6},{5,7},{6,4},{7,5}} | collective-permute-start | bytes 1572872 | tf_op jit(solution)/shard_map/ppermute | solution.py:214
  758.4 92.1 %collective-permute-start.54 = (bf16[64,128,128]{2,1,0:T(8,128)(2,1)}, bf16[64,128,128]{2,1,0:T(8,128)(2,1)}, u32[]{:S(2)}, u32[]{:S(2)}) collective-permute-start(bf16[64,128,128]{2,1,0:T(8,128)(2,1)} %get-tuple-element.463), channel_id=1, source_target_pairs={{0,4},{4,0},{1,5},{5,1},{2,6},{6,2},{3,7},{7,3}} | collective-permute-start | bytes 6291464 | tf_op jit(solution)/shard_map/ppermute | solution.py:219
  791.3 104.2 %collective-permute-start.57 = (bf16[64,128,128]{2,1,0:T(8,128)(2,1)}, bf16[64,128,128]{2,1,0:T(8,128)(2,1)}, u32[]{:S(2)}, u32[]{:S(2)}) collective-permute-start(bf16[64,128,128]{2,1,0:T(8,128)(2,1)} %get-tuple-element.472), channel_id=1, source_target_pairs={{0,4},{4,0},{1,5},{5,1},{2,6},{6,2},{3,7},{7,3}} | collective-permute-start | bytes 6291464 | tf_op jit(solution)/shard_map/ppermute | solution.py:219
  792.9 75.0 %collective-permute-start.67 = (bf16[64,64,128]{2,1,0:T(8,128)(2,1)}, bf16[64,64,128]{2,1,0:T(8,128)(2,1)}, u32[]{:S(2)}, u32[]{:S(2)}) collective-permute-start(bf16[64,64,128]{2,1,0:T(8,128)(2,1)} %get-tuple-element.490), channel_id=1, source_target_pairs={{0,3},{1,2},{2,1},{3,0},{4,7},{5,6},{6,5},{7,4}} | collective-permute-start | bytes 3145736 | tf_op jit(solution)/shard_map/ppermute | solution.py:214
  805.6 134.8 %collective-permute-start.58 = (bf16[64,128,128]{2,1,0:T(8,128)(2,1)}, bf16[64,128,128]{2,1,0:T(8,128)(2,1)}, u32[]{:S(2)}, u32[]{:S(2)}) collective-permute-start(bf16[64,128,128]{2,1,0:T(8,128)(2,1)} %get-tuple-element.475), channel_id=1, source_target_pairs={{0,4},{4,0},{1,5},{5,1},{2,6},{6,2},{3,7},{7,3}} | collective-permute-start | bytes 6291464 | tf_op jit(solution)/shard_map/ppermute | solution.py:219
  818.2 89.5 %collective-permute-start.59 = (bf16[64,64,128]{2,1,0:T(8,128)(2,1)}, bf16[64,64,128]{2,1,0:T(8,128)(2,1)}, u32[]{:S(2)}, u32[]{:S(2)}) collective-permute-start(bf16[64,64,128]{2,1,0:T(8,128)(2,1)} %get-tuple-element.478), channel_id=1, source_target_pairs={{0,1},{1,0},{2,3},{3,2},{4,5},{5,4},{6,7},{7,6}} | collective-permute-start | bytes 3145736 | tf_op jit(solution)/shard_map/ppermute | solution.py:214
  850.5 58.7 %collective-permute-start.60 = (bf16[64,64,128]{2,1,0:T(8,128)(2,1)}, bf16[64,64,128]{2,1,0:T(8,128)(2,1)}, u32[]{:S(2)}, u32[]{:S(2)}) collective-permute-start(bf16[64,64,128]{2,1,0:T(8,128)(2,1)} %get-tuple-element.479), channel_id=1, source_target_pairs={{0,2},{1,3},{2,0},{3,1},{4,6},{5,7},{6,4},{7,5}} | collective-permute-start | bytes 3145736 | tf_op jit(solution)/shard_map/ppermute | solution.py:214
  895.5 89.9 %collective-permute-start.73 = (bf16[64,128,128]{2,1,0:T(8,128)(2,1)}, bf16[64,128,128]{2,1,0:T(8,128)(2,1)}, u32[]{:S(2)}, u32[]{:S(2)}) collective-permute-start(bf16[64,128,128]{2,1,0:T(8,128)(2,1)} %get-tuple-element.506), channel_id=1, source_target_pairs={{0,4},{4,0},{1,5},{5,1},{2,6},{6,2},{3,7},{7,3}} | collective-permute-start | bytes 6291464 | tf_op jit(solution)/shard_map/ppermute | solution.py:219
  907.7 122.6 %collective-permute-start.69 = (bf16[64,128,128]{2,1,0:T(8,128)(2,1)}, bf16[64,128,128]{2,1,0:T(8,128)(2,1)}, u32[]{:S(2)}, u32[]{:S(2)}) collective-permute-start(bf16[64,128,128]{2,1,0:T(8,128)(2,1)} %get-tuple-element.497), channel_id=1, source_target_pairs={{0,4},{4,0},{1,5},{5,1},{2,6},{6,2},{3,7},{7,3}} | collective-permute-start | bytes 6291464 | tf_op jit(solution)/shard_map/ppermute | solution.py:219
  909.2 56.2 %collective-permute-start.135 = (bf16[64,64,128]{2,1,0:T(8,128)(2,1)}, bf16[64,64,128]{2,1,0:T(8,128)(2,1)}, u32[]{:S(2)}, u32[]{:S(2)}) collective-permute-start(bf16[64,64,128]{2,1,0:T(8,128)(2,1)} %get-tuple-element.630), channel_id=1, source_target_pairs={{0,1},{1,0},{2,3},{3,2},{4,5},{5,4},{6,7},{7,6}} | collective-permute-start | bytes 3145736 | tf_op jit(solution)/shard_map/ppermute | solution.py:214
  909.2 56.8 %collective-permute-start.99 = (bf16[64,64,128]{2,1,0:T(8,128)(2,1)}, bf16[64,64,128]{2,1,0:T(8,128)(2,1)}, u32[]{:S(2)}, u32[]{:S(2)}) collective-permute-start(bf16[64,64,128]{2,1,0:T(8,128)(2,1)} %get-tuple-element.557), channel_id=1, source_target_pairs={{0,1},{1,0},{2,3},{3,2},{4,5},{5,4},{6,7},{7,6}} | collective-permute-start | bytes 3145736 | tf_op jit(solution)/shard_map/ppermute | solution.py:214
  965.4 116.4 %collective-permute-start.80 = (bf16[64,128,128]{2,1,0:T(8,128)(2,1)}, bf16[64,128,128]{2,1,0:T(8,128)(2,1)}, u32[]{:S(2)}, u32[]{:S(2)}) collective-permute-start(bf16[64,128,128]{2,1,0:T(8,128)(2,1)} %get-tuple-element.519), channel_id=1, source_target_pairs={{0,4},{4,0},{1,5},{5,1},{2,6},{6,2},{3,7},{7,3}} | collective-permute-start | bytes 6291464 | tf_op jit(solution)/shard_map/ppermute | solution.py:219
  966.0 84.7 %collective-permute-start.70 = (bf16[64,64,128]{2,1,0:T(8,128)(2,1)}, bf16[64,64,128]{2,1,0:T(8,128)(2,1)}, u32[]{:S(2)}, u32[]{:S(2)}) collective-permute-start(bf16[64,64,128]{2,1,0:T(8,128)(2,1)} %get-tuple-element.500), channel_id=1, source_target_pairs={{0,1},{1,0},{2,3},{3,2},{4,5},{5,4},{6,7},{7,6}} | collective-permute-start | bytes 3145736 | tf_op jit(solution)/shard_map/ppermute | solution.py:214
  966.0 85.8 %collective-permute-start.71 = (bf16[64,64,128]{2,1,0:T(8,128)(2,1)}, bf16[64,64,128]{2,1,0:T(8,128)(2,1)}, u32[]{:S(2)}, u32[]{:S(2)}) collective-permute-start(bf16[64,64,128]{2,1,0:T(8,128)(2,1)} %get-tuple-element.501), channel_id=1, source_target_pairs={{0,2},{1,3},{2,0},{3,1},{4,6},{5,7},{6,4},{7,5}} | collective-permute-start | bytes 3145736 | tf_op jit(solution)/shard_map/ppermute | solution.py:214
  985.4 67.5 %collective-permute-start.72 = (bf16[64,64,128]{2,1,0:T(8,128)(2,1)}, bf16[64,64,128]{2,1,0:T(8,128)(2,1)}, u32[]{:S(2)}, u32[]{:S(2)}) collective-permute-start(bf16[64,64,128]{2,1,0:T(8,128)(2,1)} %get-tuple-element.502), channel_id=1, source_target_pairs={{0,3},{1,2},{2,1},{3,0},{4,7},{5,6},{6,5},{7,4}} | collective-permute-start | bytes 3145736 | tf_op jit(solution)/shard_map/ppermute | solution.py:214
  1030.3 48.2 %collective-permute-start.101 = (bf16[64,64,128]{2,1,0:T(8,128)(2,1)}, bf16[64,64,128]{2,1,0:T(8,128)(2,1)}, u32[]{:S(2)}, u32[]{:S(2)}) collective-permute-start(bf16[64,64,128]{2,1,0:T(8,128)(2,1)} %get-tuple-element.559), channel_id=1, source_target_pairs={{0,3},{1,2},{2,1},{3,0},{4,7},{5,6},{6,5},{7,4}} | collective-permute-start | bytes 3145736 | tf_op jit(solution)/shard_map/ppermute | solution.py:214
  1079.1 48.3 %collective-permute-start.94 = (bf16[32,128,128]{2,1,0:T(8,128)(2,1)}, bf16[32,128,128]{2,1,0:T(8,128)(2,1)}, u32[]{:S(2)}, u32[]{:S(2)}) collective-permute-start(bf16[32,128,128]{2,1,0:T(8,128)(2,1)} %get-tuple-element.546), channel_id=1, source_target_pairs={{0,4},{4,0},{1,5},{5,1},{2,6},{6,2},{3,7},{7,3}} | collective-permute-start | bytes 3145736 | tf_op jit(solution)/shard_map/ppermute | solution.py:219
  1080.6 47.8 %collective-permute-start.81 = (bf16[64,64,128]{2,1,0:T(8,128)(2,1)}, bf16[64,64,128]{2,1,0:T(8,128)(2,1)}, u32[]{:S(2)}, u32[]{:S(2)}) collective-permute-start(bf16[64,64,128]{2,1,0:T(8,128)(2,1)} %get-tuple-element.522), channel_id=1, source_target_pairs={{0,1},{1,0},{2,3},{3,2},{4,5},{5,4},{6,7},{7,6}} | collective-permute-start | bytes 3145736 | tf_op jit(solution)/shard_map/ppermute | solution.py:214
  1080.8 47.6 %collective-permute-start.82 = (bf16[64,64,128]{2,1,0:T(8,128)(2,1)}, bf16[64,64,128]{2,1,0:T(8,128)(2,1)}, u32[]{:S(2)}, u32[]{:S(2)}) collective-permute-start(bf16[64,64,128]{2,1,0:T(8,128)(2,1)} %get-tuple-element.523), channel_id=1, source_target_pairs={{0,2},{1,3},{2,0},{3,1},{4,6},{5,7},{6,4},{7,5}} | collective-permute-start | bytes 3145736 | tf_op jit(solution)/shard_map/ppermute | solution.py:214
  1081.8 47.6 %collective-permute-start.83 = (bf16[64,64,128]{2,1,0:T(8,128)(2,1)}, bf16[64,64,128]{2,1,0:T(8,128)(2,1)}, u32[]{:S(2)}, u32[]{:S(2)}) collective-permute-start(bf16[64,64,128]{2,1,0:T(8,128)(2,1)} %get-tuple-element.524), channel_id=1, source_target_pairs={{0,3},{1,2},{2,1},{3,0},{4,7},{5,6},{6,5},{7,4}} | collective-permute-start | bytes 3145736 | tf_op jit(solution)/shard_map/ppermute | solution.py:214
  1104.9 121.3 %collective-permute-start.107 = (bf16[64,128,128]{2,1,0:T(8,128)(2,1)}, bf16[64,128,128]{2,1,0:T(8,128)(2,1)}, u32[]{:S(2)}, u32[]{:S(2)}) collective-permute-start(bf16[64,128,128]{2,1,0:T(8,128)(2,1)} %get-tuple-element.575), channel_id=1, source_target_pairs={{0,4},{4,0},{1,5},{5,1},{2,6},{6,2},{3,7},{7,3}} | collective-permute-start | bytes 6291464 | tf_op jit(solution)/shard_map/ppermute | solution.py:219
  1127.4 53.0 %collective-permute-start.136 = (bf16[64,64,128]{2,1,0:T(8,128)(2,1)}, bf16[64,64,128]{2,1,0:T(8,128)(2,1)}, u32[]{:S(2)}, u32[]{:S(2)}) collective-permute-start(bf16[64,64,128]{2,1,0:T(8,128)(2,1)} %get-tuple-element.631), channel_id=1, source_target_pairs={{0,2},{1,3},{2,0},{3,1},{4,6},{5,7},{6,4},{7,5}} | collective-permute-start | bytes 3145736 | tf_op jit(solution)/shard_map/ppermute | solution.py:214
  1128.4 52.3 %collective-permute-start.104 = (bf16[64,64,128]{2,1,0:T(8,128)(2,1)}, bf16[64,64,128]{2,1,0:T(8,128)(2,1)}, u32[]{:S(2)}, u32[]{:S(2)}) collective-permute-start(bf16[64,64,128]{2,1,0:T(8,128)(2,1)} %get-tuple-element.569), channel_id=1, source_target_pairs={{0,1},{1,0},{2,3},{3,2},{4,5},{5,4},{6,7},{7,6}} | collective-permute-start | bytes 3145736 | tf_op jit(solution)/shard_map/ppermute | solution.py:214
  1128.4 56.2 %collective-permute-start.105 = (bf16[64,64,128]{2,1,0:T(8,128)(2,1)}, bf16[64,64,128]{2,1,0:T(8,128)(2,1)}, u32[]{:S(2)}, u32[]{:S(2)}) collective-permute-start(bf16[64,64,128]{2,1,0:T(8,128)(2,1)} %get-tuple-element.570), channel_id=1, source_target_pairs={{0,2},{1,3},{2,0},{3,1},{4,6},{5,7},{6,4},{7,5}} | collective-permute-start | bytes 3145736 | tf_op jit(solution)/shard_map/ppermute | solution.py:214
  1129.4 67.8 %collective-permute-start.106 = (bf16[64,64,128]{2,1,0:T(8,128)(2,1)}, bf16[64,64,128]{2,1,0:T(8,128)(2,1)}, u32[]{:S(2)}, u32[]{:S(2)}) collective-permute-start(bf16[64,64,128]{2,1,0:T(8,128)(2,1)} %get-tuple-element.571), channel_id=1, source_target_pairs={{0,3},{1,2},{2,1},{3,0},{4,7},{5,6},{6,5},{7,4}} | collective-permute-start | bytes 3145736 | tf_op jit(solution)/shard_map/ppermute | solution.py:214
  1217.2 52.4 %collective-permute-start.109 = (bf16[32,128,128]{2,1,0:T(8,128)(2,1)}, bf16[32,128,128]{2,1,0:T(8,128)(2,1)}, u32[]{:S(2)}, u32[]{:S(2)}) collective-permute-start(bf16[32,128,128]{2,1,0:T(8,128)(2,1)} %get-tuple-element.581), channel_id=1, source_target_pairs={{0,4},{4,0},{1,5},{5,1},{2,6},{6,2},{3,7},{7,3}} | collective-permute-start | bytes 3145736 | tf_op jit(solution)/shard_map/ppermute | solution.py:219
  1224.6 67.4 %collective-permute-start.128 = (bf16[32,128,128]{2,1,0:T(8,128)(2,1)}, bf16[32,128,128]{2,1,0:T(8,128)(2,1)}, u32[]{:S(2)}, u32[]{:S(2)}) collective-permute-start(bf16[32,128,128]{2,1,0:T(8,128)(2,1)} %get-tuple-element.612), channel_id=1, source_target_pairs={{0,4},{4,0},{1,5},{5,1},{2,6},{6,2},{3,7},{7,3}} | collective-permute-start | bytes 3145736 | tf_op jit(solution)/shard_map/ppermute | solution.py:219
  1241.9 92.7 %collective-permute-start.129 = (bf16[64,64,128]{2,1,0:T(8,128)(2,1)}, bf16[64,64,128]{2,1,0:T(8,128)(2,1)}, u32[]{:S(2)}, u32[]{:S(2)}) collective-permute-start(bf16[64,64,128]{2,1,0:T(8,128)(2,1)} %get-tuple-element.615), channel_id=1, source_target_pairs={{0,1},{1,0},{2,3},{3,2},{4,5},{5,4},{6,7},{7,6}} | collective-permute-start | bytes 3145736 | tf_op jit(solution)/shard_map/ppermute | solution.py:214
  1246.5 89.1 %collective-permute-start.130 = (bf16[64,64,128]{2,1,0:T(8,128)(2,1)}, bf16[64,64,128]{2,1,0:T(8,128)(2,1)}, u32[]{:S(2)}, u32[]{:S(2)}) collective-permute-start(bf16[64,64,128]{2,1,0:T(8,128)(2,1)} %get-tuple-element.616), channel_id=1, source_target_pairs={{0,2},{1,3},{2,0},{3,1},{4,6},{5,7},{6,4},{7,5}} | collective-permute-start | bytes 3145736 | tf_op jit(solution)/shard_map/ppermute | solution.py:214
  1247.6 89.1 %collective-permute-start.131 = (bf16[64,64,128]{2,1,0:T(8,128)(2,1)}, bf16[64,64,128]{2,1,0:T(8,128)(2,1)}, u32[]{:S(2)}, u32[]{:S(2)}) collective-permute-start(bf16[64,64,128]{2,1,0:T(8,128)(2,1)} %get-tuple-element.617), channel_id=1, source_target_pairs={{0,3},{1,2},{2,1},{3,0},{4,7},{5,6},{6,5},{7,4}} | collective-permute-start | bytes 3145736 | tf_op jit(solution)/shard_map/ppermute | solution.py:214
  1269.6 67.5 %collective-permute-start.132 = (bf16[32,128,128]{2,1,0:T(8,128)(2,1)}, bf16[32,128,128]{2,1,0:T(8,128)(2,1)}, u32[]{:S(2)}, u32[]{:S(2)}) collective-permute-start(bf16[32,128,128]{2,1,0:T(8,128)(2,1)} %get-tuple-element.621), channel_id=1, source_target_pairs={{0,4},{4,0},{1,5},{5,1},{2,6},{6,2},{3,7},{7,3}} | collective-permute-start | bytes 3145736 | tf_op jit(solution)/shard_map/ppermute | solution.py:219
  (103 other events, 2324.3 us)
where the time goes:
time: 1450 us; the launch traced here: 1440 us
  waiting for transfers between devices  762 us (53%)
  Pallas kernels  547 us (38%)
  starting transfers between devices  119 us (8%)
    pallas_call x84, Pallas kernels, call(): pl.pallas_call(wrapped, grid=grid, in_specs=[any_spec()] + list(in_specs)...  547 us
    ppermute x40, waiting for transfers between devices, over_col(): return lax.ppermute(value, 'col', [(0, 1), (1, 0)])  458 us
    ppermute x120, waiting for transfers between devices, over_row(): got[k] = lax.ppermute(outs[k], 'row', [(r, r ^ k) for r in range(4)])  304 us
    ppermute x120, starting transfers between devices, over_row(): got[k] = lax.ppermute(outs[k], 'row', [(r, r ^ k) for r in range(4)])  82.8 us
    ppermute x40, starting transfers between devices, over_col(): return lax.ppermute(value, 'col', [(0, 1), (1, 0)])  36.3 us
  transfers between devices with their start and end apart: 160, of which 51 were waited for; matrix products, arithmetic and copies ran while one was open for 1% of the time, Pallas kernels for 37%

commit v1 on v0

--- a/solution.py
+++ b/solution.py
@@ -8,10 +8,9 @@
 
 BF = jnp.bfloat16
 F32 = jnp.float32
-UNROLL = 2
 
 SLABS = (
-    (8, 8, 16, 32,),
+    (8, 16, 16, 24,),
     (32, 32,),
     (64,),
     (64,),
@@ -22,21 +21,22 @@
     (64,),
     (64,),
     (32, 32,),
-    (32, 16, 8, 8,),
+    (16, 16, 16, 8, 8,),
 )
 
 
 ORDER = (
-    (1, 0, (0, 1, 2, 3)), (2, 0, 1), (2, 0, 0), (3, 0, 1), (2, 0, 2), (3, 0, 0), (1, 1, (0, 1)), (3, 0, 2),
-    (2, 0, 3), (1, 8, (0,)), (2, 1, 0), (2, 1, 1), (1, 4, (0,)), (1, 3, (0,)), (3, 0, 3), (1, 5, (0,)),
-    (3, 1, 0), (2, 8, 0), (3, 1, 1), (2, 3, 0), (1, 6, (0,)), (2, 4, 0), (3, 8, 0), (1, 11, (0, 1, 2, 3)),
-    (1, 10, (0, 1)), (3, 4, 0), (1, 9, (0,)), (2, 6, 0), (2, 5, 0), (1, 2, (0,)), (5, 4, 0), (2, 2, 0),
-    (3, 5, 0), (5, 0, 1), (5, 1, 1), (1, 7, (0,)), (3, 3, 0), (3, 2, 0), (2, 7, 0), (5, 5, 0), (5, 3, 0),
-    (5, 8, 0), (3, 6, 0), (3, 7, 0), (5, 2, 0), (6, 5, 0), (2, 9, 0), (6, 4, 0), (5, 1, 0), (5, 7, 0),
-    (6, 2, 0), (5, 6, 0), (2, 10, 1), (2, 10, 0), (3, 9, 0), (6, 7, 0), (6, 1, 0), (5, 0, 3), (2, 11, 0),
-    (3, 10, 1), (2, 11, 2), (5, 0, 0), (6, 3, 0), (3, 10, 0), (5, 0, 2), (6, 6, 0), (5, 9, 0), (3, 11, 0),
-    (5, 10, 1), (2, 11, 3), (6, 0, 0), (2, 11, 1), (5, 10, 0), (6, 9, 0), (5, 11, 0), (3, 11, 2), (3, 11, 3),
-    (6, 8, 0), (3, 11, 1), (5, 11, 2), (5, 11, 3), (5, 11, 1), (6, 10, 0), (6, 11, 0),
+    (1, 0, (0, 1, 2, 3)), (0, 0, 0), (2, 0, 0), (2, 0, 1), (3, 0, 0), (2, 0, 2), (3, 0, 1), (1, 1, (0, 1)),
+    (2, 0, 3), (3, 0, 2), (2, 1, 0), (5, 0, 1), (3, 0, 3), (5, 0, 2), (1, 2, (0,)), (5, 0, 0), (2, 1, 1),
+    (3, 1, 0), (5, 0, 3), (2, 2, 0), (1, 3, (0,)), (3, 1, 1), (1, 4, (0,)), (5, 1, 0), (6, 0, 0),
+    (1, 5, (0,)), (2, 3, 0), (3, 2, 0), (5, 1, 1), (3, 3, 0), (5, 2, 0), (2, 4, 0), (5, 3, 0), (6, 1, 0),
+    (1, 6, (0,)), (2, 5, 0), (3, 4, 0), (6, 2, 0), (3, 5, 0), (1, 7, (0,)), (6, 3, 0), (5, 4, 0), (2, 6, 0),
+    (5, 5, 0), (1, 8, (0,)), (2, 7, 0), (3, 6, 0), (1, 9, (0,)), (6, 4, 0), (2, 8, 0), (3, 7, 0), (5, 6, 0),
+    (1, 10, (0, 1)), (2, 9, 0), (6, 6, 0), (3, 8, 0), (5, 7, 0), (2, 10, 0), (3, 9, 0), (5, 8, 0), (6, 5, 0),
+    (6, 7, 0), (1, 11, (0, 1, 2, 3, 4)), (3, 10, 0), (2, 10, 1), (2, 11, 1), (5, 9, 0), (6, 8, 0), (2, 11, 0),
+    (3, 10, 1), (5, 10, 0), (6, 9, 0), (3, 11, 0), (5, 10, 1), (2, 11, 2), (3, 11, 1), (5, 11, 0), (2, 11, 3),
+    (3, 11, 2), (6, 10, 0), (5, 11, 1), (2, 11, 4), (3, 11, 3), (5, 11, 2), (3, 11, 4), (5, 11, 3),
+    (5, 11, 4), (6, 11, 0),
 )
 
 
@@ -52,39 +52,73 @@
     return pl.BlockSpec(shape, lambda *g: (0,) * len(shape))
 
 
-def call(body, token, ins, in_specs, outs, out_specs, grid, flops, alias=None):
-    n_in, n_out = len(ins), len(outs)
-
-    def wrapped(token_ref, *refs):
-        body(refs[:n_in], refs[n_in:n_in + n_out])
-
-    aliases = {0: n_out}
-    aliases.update(alias or {})
+TOKEN = jax.ShapeDtypeStruct((8, 128), F32)
+
+
+def call(body, token, ins, in_specs, outs, out_specs, grid, flops, alias=None, scratch=()):
+    n_in, n_out, lead = len(ins), len(outs), 0 if token is None else 1
+
+    def wrapped(*refs):
+        refs = refs[lead:]
+        body(refs[:n_in], refs[n_in:n_in + n_out], *refs[n_in + n_out + 1:])
+
+    aliases = {i + lead: o for i, o in (alias or {}).items()}
+    if lead:
+        aliases[0] = n_out
     results = pl.pallas_call(
         wrapped,
         grid=grid,
-        in_specs=[any_spec()] + list(in_specs),
+        in_specs=[any_spec()] * lead + list(in_specs),
         out_specs=list(out_specs) + [any_spec()],
-        out_shape=list(outs) + [jax.ShapeDtypeStruct(token.shape, token.dtype)],
+        out_shape=list(outs) + [TOKEN],
         input_output_aliases=aliases,
+        scratch_shapes=list(scratch),
         cost_estimate=pl.CostEstimate(flops=flops, bytes_accessed=1 << 20, transcendentals=0),
         compiler_params=pltpu.CompilerParams(vmem_limit_bytes=67043328),
-    )(token, *ins)
+    )(*([token] * lead), *ins)
     return results[:-1], results[-1]
 
 
-def stage_one(token, u, a4, b, parts, ny, nz, yb=16, sub=8):
+def peer_rows(ref, me, k, size, offset=0, count=None):
+    at = pl.multiple_of((me ^ k) * size, size) + offset
+    return ref[pl.ds(at, count or size), :]
+
+
+def prepare(token, a, bm, cm):
+    n = a.shape[0]
+
+    def body(ins, outs, rows):
+        a_ref, b_ref, c_ref = ins
+        a6, b4, b5, c_in, c_out = outs
+        r, c = lax.axis_index("row"), lax.axis_index("col")
+        a6[...] = jnp.concatenate([peer_rows(a_ref, r, k, n // 4) for k in range(4)], axis=0).T
+        rows[...] = jnp.concatenate([peer_rows(b_ref, c, l, n // 2) for l in range(2)], axis=0).T
+        back = jnp.concatenate([peer_rows(rows, r, k, n // 4) for k in range(4)], axis=0)
+        b5[...] = back
+        b4[...] = back.T
+        half = n // 2
+        out = jnp.concatenate([c_ref[:, pl.ds(pl.multiple_of((c ^ l) * half, half), half)] for l in range(2)], axis=1)
+        c_out[...] = out
+        c_in[...] = out.T
+
+    spec = whole((n, n))
+    return call(body, token, (a, bm, cm), [spec] * 3, [jax.ShapeDtypeStruct((n, n), BF)] * 5, [spec] * 5, (1,),
+                1 << 20, scratch=[pltpu.VMEM((n, n), BF)])
+
+
+def stage_one(token, u, a, b, parts, ny, nz, yb=16, sub=8):
     nx = u.shape[1]
     rows = 4 * sum(s for _, s in parts)
 
     def body(ins, outs):
         u_ref, a_ref = ins
-        a = jnp.concatenate([a_ref[k, o:o + s, :] for o, s in parts for k in range(4)], axis=0)
+        r = lax.axis_index("row")
+        mine = jnp.concatenate([peer_rows(a_ref, r, k, nx // 4, o, s) for o, s in parts for k in range(4)], axis=0)
 
         def step(t, carry):
             at_y = pl.ds(pl.multiple_of(t * sub, sub), sub)
             flat = u_ref[0, :, at_y, :].reshape(nx, sub * nz)
-            h = dot(a, flat).astype(BF).reshape(rows, sub, nz)
+            h = dot(mine, flat).astype(BF).reshape(rows, sub, nz)
             at = 0
             for n, (o, s) in enumerate(parts):
                 for k in range(4):
@@ -96,12 +130,17 @@
 
     outs = [jax.ShapeDtypeStruct((s, ny, nz), BF) for _, s in parts for _ in range(4)]
     out_specs = [pl.BlockSpec((s, yb, nz), lambda g: (0, g, 0)) for _, s in parts for _ in range(4)]
-    return call(body, token, (u, a4), [pl.BlockSpec((1, nx, yb, nz), lambda g: (b, 0, g, 0)), whole(a4.shape)],
+    return call(body, token, (u, a), [pl.BlockSpec((1, nx, yb, nz), lambda g: (b, 0, g, 0)), whole(a.shape)],
                 outs, out_specs, (ny // yb,), 2 * rows * nx * ny * nz)
 
 
-def stage_two(token, pieces, b4, ti=8):
+def block_of(size):
+    return 16 if size % 16 == 0 else 8
+
+
+def stage_two(token, pieces, b4):
     size, ny, nz = pieces[0].shape
+    ti = block_of(size)
     nj = b4.shape[0] // 2
 
     def body(ins, outs):
@@ -116,7 +155,7 @@
                     outs[l][i + e] = h[l * nj:(l + 1) * nj, e * nz:(e + 1) * nz]
             return carry
 
-        lax.fori_loop(0, ti // 2, step, 0, unroll=UNROLL)
+        lax.fori_loop(0, ti // 2, step, 0, unroll=4 if size <= 8 else 2)
 
     out = jax.ShapeDtypeStruct((size, nj, nz), BF)
     return call(body, token, (*pieces, b4), [pl.BlockSpec((ti, ny, nz), lambda g: (g, 0, 0))] * 4 + [whole(b4.shape)],
@@ -124,8 +163,9 @@
                 2 * size * 4 * ny * 2 * nj * nz)
 
 
-def stage_three_four(token, own, got, c_in, c_out, diag, offset, ti=8):
+def stage_three_four(token, own, got, c_in, c_out, diag, offset):
     size, nj, nz = own.shape
+    ti = block_of(size if offset % 16 == 0 else 8)
     nk = c_out.shape[0]
 
     def body(ins, outs):
@@ -142,7 +182,7 @@
                     outs[l][i + e] = h4[e * nj:(e + 1) * nj, l * nz:(l + 1) * nz]
             return carry
 
-        lax.fori_loop(0, ti // 2, step, 0, unroll=UNROLL)
+        lax.fori_loop(0, ti // 2, step, 0, unroll=4 if size <= 8 else 2)
 
     first = offset // ti
     block = pl.BlockSpec((ti, nj, nz), lambda g: (g, 0, 0))
@@ -152,8 +192,9 @@
                 [out] * 2, [block] * 2, (size // ti,), 4 * size * nj * 2 * nz * nk)
 
 
-def stage_five(token, own, got, b5, ti=8):
+def stage_five(token, own, got, b5):
     size, nj, nz = own.shape
+    ti = block_of(size)
     ny = b5.shape[0] // 4
 
     def body(ins, outs):
@@ -168,7 +209,7 @@
                     outs[k][i + e] = h[k * ny:(k + 1) * ny, e * nz:(e + 1) * nz]
             return carry
 
-        lax.fori_loop(0, ti // 2, step, 0, unroll=UNROLL)
+        lax.fori_loop(0, ti // 2, step, 0, unroll=4 if size <= 8 else 2)
 
     out = jax.ShapeDtypeStruct((size, ny, nz), BF)
     return call(body, token, (own, got, b5), [pl.BlockSpec((ti, nj, nz), lambda g: (g, 0, 0))] * 2 + [whole(b5.shape)],
@@ -196,7 +237,7 @@
     if w is not None:
         ins += (w,)
         in_specs.append(any_spec())
-        alias = {len(ins): 0}
+        alias = {len(ins) - 1: 0}
     (w,), token = call(body, token, ins, in_specs, [jax.ShapeDtypeStruct((batch, nx, ny, nz), F32)],
                        [pl.BlockSpec((1, nx, yb, nz), lambda g: (b, 0, g, 0))], (ny // yb,),
                        2 * nx * nx * ny * nz, alias)
@@ -219,19 +260,8 @@
         return lax.ppermute(value, "col", [(0, 1), (1, 0)])
 
     def local_apply(u, a, bm, cm, diag):
-        batch, nx, ny, nz = u.shape
-        r, c = lax.axis_index("row"), lax.axis_index("col")
-        peers = jnp.bitwise_xor(r, jnp.arange(4))
-        sides = jnp.bitwise_xor(c, jnp.arange(2))
-        slab = nx // 4
-        a4 = jnp.take(a.reshape(4, slab, nx), peers, axis=0)
-        a6 = a4.reshape(nx, nx).T
-        b4 = jnp.take(bm.reshape(2, nx // 2, 4, nx // 4), sides, axis=0)
-        b4 = jnp.take(b4, peers, axis=2).reshape(nx, nx)
-        b5 = b4.T
-        c_out = jnp.take(cm.reshape(nx, 2, nx // 2), sides, axis=1).reshape(nx, nx)
-        c_in = c_out.T
-        token = jnp.zeros((8, 128), F32)
+        batch, _, ny, nz = u.shape
+        token = None
         cuts = SLABS
         starts = [[sum(cut[:q]) for q in range(len(cut))] for cut in cuts]
         y_in, z_in, j_in, x_in = {}, {}, {}, {}
@@ -239,9 +269,11 @@
         for kind, b, q in ORDER:
             if kind == 1:
                 parts = [(starts[b][p], cuts[b][p]) for p in q]
-                outs, token = stage_one(token, u, a4, b, parts, ny, nz)
+                outs, token = stage_one(token, u, a, b, parts, ny, nz)
                 for m, part in enumerate(q):
                     y_in[b, part] = over_row(outs[4 * m:4 * m + 4], 3 * m)
+            elif kind == 0:
+                (a6, b4, b5, c_in, c_out), token = prepare(token, a, bm, cm)
             elif kind == 2:
                 (own, other), token = stage_two(token, y_in.pop((b, q)), b4)
                 z_in[b, q] = (own, over_col(other))

time: 1450 us -> 1360 us (0.938)
  waiting for transfers between devices: 762 us -> 697 us
  Pallas kernels: 547 us -> 516 us
  starting transfers between devices: 119 us -> 142 us
    ppermute x40 -> x42, waiting for transfers between devices: 458 us -> 184 us  [over_col(): return lax.ppermute(value, 'col', [(0, 1), (1, 0)])]
    ppermute x120 -> x126, waiting for transfers between devices: 304 us -> 513 us  [over_row(): got[k] = lax.ppermute(outs[k], 'row', [(r, r ^ k) for r in range(4)])]
    pallas_call x84 -> x88, Pallas kernels: 547 us -> 516 us  [call(): pl.pallas_call(wrapped, grid=grid, in_specs=[any_spec()] * lead + list(in...]
    ppermute x120 -> x126, starting transfers between devices: 82.8 us -> 97.1 us  [over_row(): got[k] = lax.ppermute(outs[k], 'row', [(r, r ^ k) for r in range(4)])]
    ppermute x40 -> x42, starting transfers between devices: 36.3 us -> 45.4 us  [over_col(): return lax.ppermute(value, 'col', [(0, 1), (1, 0)])]
  transfers between devices with their start and end apart: 160 -> 168, of which waited for: 51 -> 62; matrix products, arithmetic and copies ran while one was open for 1% -> 0% of each run, Pallas kernels for 37% -> 37%
where the time goes in v1:
time: 1360 us
  waiting for transfers between devices  697 us (51%)
  Pallas kernels  516 us (38%)
  starting transfers between devices  142 us (10%)
    pallas_call x88, Pallas kernels, call(): pl.pallas_call(wrapped, grid=grid, in_specs=[any_spec()] * lead + list(in...  516 us
    ppermute x126, waiting for transfers between devices, over_row(): got[k] = lax.ppermute(outs[k], 'row', [(r, r ^ k) for r in range(4)])  513 us
    ppermute x42, waiting for transfers between devices, over_col(): return lax.ppermute(value, 'col', [(0, 1), (1, 0)])  184 us
    ppermute x126, starting transfers between devices, over_row(): got[k] = lax.ppermute(outs[k], 'row', [(r, r ^ k) for r in range(4)])  97.1 us
    ppermute x42, starting transfers between devices, over_col(): return lax.ppermute(value, 'col', [(0, 1), (1, 0)])  45.4 us
  transfers between devices with their start and end apart: 168, of which 62 were waited for; matrix products, arithmetic and copies ran while one was open for 0% of the time, Pallas kernels for 37%

profile of v1, /device:TPU:0, one launch (start us, length us, event | category | flops | bytes accessed | tf_op | source)
XLA Modules:
  0.0 1355.7 jit_solution(96637373457025606)
XLA Ops:
  0.0 6.9 shard_map.55
  14.5 12.1 collective-permute-done.1.refs_3_
  37.8 7.1 collective-permute-done.8.refs_3_
  46.4 7.3 collective-permute-done.6.refs_2_
  75.9 16.6 %collective-permute-done.21.refs_2_ = bf16[8,128,128]{2,1,0:T(8,128)(2,1)} collective-permute-done((bf16[8,128,128]{2,1,0:T(8,128)(2,1)}, bf16[8,128,128]{2,1,0:T(8,128)(2,1)}, u32[]{:S(2)}, u32[]{:S(2)}) %collective-permute-start.21) | collective-permute-done | bytes 262176 | tf_op jit(solution)/shard_map/ppermute | solution.py:260
  118.4 10.8 collective-permute-done.20.refs_2_
  185.5 18.2 %collective-permute-done.29.refs_4_ = bf16[64,64,128]{2,1,0:T(8,128)(2,1)} collective-permute-done((bf16[64,64,128]{2,1,0:T(8,128)(2,1)}, bf16[64,64,128]{2,1,0:T(8,128)(2,1)}, u32[]{:S(2)}, u32[]{:S(2)}) %collective-permute-start.29) | collective-permute-done | bytes 1048608 | tf_op jit(solution)/shard_map/ppermute | solution.py:255
  205.9 6.9 shard_map.74
  213.2 6.9 shard_map.75
  242.1 34.3 %collective-permute-done.43.refs_16_ = bf16[24,64,128]{2,1,0:T(8,128)(2,1)} collective-permute-done((bf16[24,64,128]{2,1,0:T(8,128)(2,1)}, bf16[24,64,128]{2,1,0:T(8,128)(2,1)}, u32[]{:S(2)}, u32[]{:S(2)}) %collective-permute-start.43) | collective-permute-done | bytes 393248 | tf_op jit(solution)/shard_map/ppermute | solution.py:255
  276.4 7.9 shard_map.79
  284.3 6.8 shard_map.80
  291.1 6.9 shard_map.81
  300.0 10.6 shard_map.82
  312.2 57.0 %collective-permute-done.48.refs_2_ = bf16[32,128,128]{2,1,0:T(8,128)(2,1)} collective-permute-done((bf16[32,128,128]{2,1,0:T(8,128)(2,1)}, bf16[32,128,128]{2,1,0:T(8,128)(2,1)}, u32[]{:S(2)}, u32[]{:S(2)}) %collective-permute-start.48) | collective-permute-done | bytes 1048608 | tf_op jit(solution)/shard_map/ppermute | solution.py:260
  373.4 10.6 shard_map.84
  387.7 24.2 %collective-permute-done.52.refs_3_ = bf16[64,64,128]{2,1,0:T(8,128)(2,1)} collective-permute-done((bf16[64,64,128]{2,1,0:T(8,128)(2,1)}, bf16[64,64,128]{2,1,0:T(8,128)(2,1)}, u32[]{:S(2)}, u32[]{:S(2)}) %collective-permute-start.52) | collective-permute-done | bytes 1048608 | tf_op jit(solution)/shard_map/ppermute | solution.py:255
  413.4 20.0 %collective-permute-done.53.refs_4_ = bf16[64,64,128]{2,1,0:T(8,128)(2,1)} collective-permute-done((bf16[64,64,128]{2,1,0:T(8,128)(2,1)}, bf16[64,64,128]{2,1,0:T(8,128)(2,1)}, u32[]{:S(2)}, u32[]{:S(2)}) %collective-permute-start.53) | collective-permute-done | bytes 1048608 | tf_op jit(solution)/shard_map/ppermute | solution.py:255
  442.8 6.9 shard_map.86
  458.5 9.6 collective-permute-done.58.refs_6_
  476.5 44.3 %collective-permute-done.60.refs_8_ = bf16[32,64,128]{2,1,0:T(8,128)(2,1)} collective-permute-done((bf16[32,64,128]{2,1,0:T(8,128)(2,1)}, bf16[32,64,128]{2,1,0:T(8,128)(2,1)}, u32[]{:S(2)}, u32[]{:S(2)}) %collective-permute-start.60) | collective-permute-done | bytes 524320 | tf_op jit(solution)/shard_map/ppermute | solution.py:255
  521.6 7.8 shard_map.88
  529.4 6.8 shard_map.89
  537.8 6.9 shard_map.90
  545.2 10.5 shard_map.91
  564.1 20.0 %collective-permute-done.67.refs_4_ = bf16[64,64,128]{2,1,0:T(8,128)(2,1)} collective-permute-done((bf16[64,64,128]{2,1,0:T(8,128)(2,1)}, bf16[64,64,128]{2,1,0:T(8,128)(2,1)}, u32[]{:S(2)}, u32[]{:S(2)}) %collective-permute-start.67) | collective-permute-done | bytes 1048608 | tf_op jit(solution)/shard_map/ppermute | solution.py:255
  586.3 21.2 %collective-permute-done.70.refs_3_ = bf16[64,64,128]{2,1,0:T(8,128)(2,1)} collective-permute-done((bf16[64,64,128]{2,1,0:T(8,128)(2,1)}, bf16[64,64,128]{2,1,0:T(8,128)(2,1)}, u32[]{:S(2)}, u32[]{:S(2)}) %collective-permute-start.70) | collective-permute-done | bytes 1048608 | tf_op jit(solution)/shard_map/ppermute | solution.py:255
  609.0 7.5 shard_map.92
  616.5 10.6 shard_map.93
  634.5 7.5 shard_map.95
  652.5 20.6 %collective-permute-done.75.refs_4_ = bf16[64,64,128]{2,1,0:T(8,128)(2,1)} collective-permute-done((bf16[64,64,128]{2,1,0:T(8,128)(2,1)}, bf16[64,64,128]{2,1,0:T(8,128)(2,1)}, u32[]{:S(2)}, u32[]{:S(2)}) %collective-permute-start.75) | collective-permute-done | bytes 1048608 | tf_op jit(solution)/shard_map/ppermute | solution.py:255
  673.1 6.9 shard_map.97
  684.1 23.3 %collective-permute-done.78.refs_3_ = bf16[64,64,128]{2,1,0:T(8,128)(2,1)} collective-permute-done((bf16[64,64,128]{2,1,0:T(8,128)(2,1)}, bf16[64,64,128]{2,1,0:T(8,128)(2,1)}, u32[]{:S(2)}, u32[]{:S(2)}) %collective-permute-start.78) | collective-permute-done | bytes 1048608 | tf_op jit(solution)/shard_map/ppermute | solution.py:255
  729.1 6.8 shard_map.100
  737.4 10.6 shard_map.101
  754.0 20.0 %collective-permute-done.83.refs_4_ = bf16[64,64,128]{2,1,0:T(8,128)(2,1)} collective-permute-done((bf16[64,64,128]{2,1,0:T(8,128)(2,1)}, bf16[64,64,128]{2,1,0:T(8,128)(2,1)}, u32[]{:S(2)}, u32[]{:S(2)}) %collective-permute-start.83) | collective-permute-done | bytes 1048608 | tf_op jit(solution)/shard_map/ppermute | solution.py:255
  783.0 14.3 %collective-permute-done.85.refs_3_ = bf16[64,64,128]{2,1,0:T(8,128)(2,1)} collective-permute-done((bf16[64,64,128]{2,1,0:T(8,128)(2,1)}, bf16[64,64,128]{2,1,0:T(8,128)(2,1)}, u32[]{:S(2)}, u32[]{:S(2)}) %collective-permute-start.85) | collective-permute-done | bytes 1048608 | tf_op jit(solution)/shard_map/ppermute | solution.py:255
  799.0 20.0 %collective-permute-done.86.refs_4_ = bf16[64,64,128]{2,1,0:T(8,128)(2,1)} collective-permute-done((bf16[64,64,128]{2,1,0:T(8,128)(2,1)}, bf16[64,64,128]{2,1,0:T(8,128)(2,1)}, u32[]{:S(2)}, u32[]{:S(2)}) %collective-permute-start.86) | collective-permute-done | bytes 1048608 | tf_op jit(solution)/shard_map/ppermute | solution.py:255
  821.2 7.5 shard_map.103
  828.6 6.9 shard_map.104
  837.1 10.6 shard_map.105
  856.3 7.6 collective-permute-done.91.refs_4_
  865.4 6.9 shard_map.107
  872.3 6.8 shard_map.108
  879.7 7.6 collective-permute-done.93.refs_3_
  887.2 20.6 %collective-permute-done.94.refs_4_ = bf16[64,64,128]{2,1,0:T(8,128)(2,1)} collective-permute-done((bf16[64,64,128]{2,1,0:T(8,128)(2,1)}, bf16[64,64,128]{2,1,0:T(8,128)(2,1)}, u32[]{:S(2)}, u32[]{:S(2)}) %collective-permute-start.94) | collective-permute-done | bytes 1048608 | tf_op jit(solution)/shard_map/ppermute | solution.py:255
  909.4 7.5 shard_map.109
  917.7 10.6 shard_map.110
  949.4 10.1 collective-permute-done.99.refs_4_
  960.5 13.8 %collective-permute-done.100.refs_2_ = bf16[64,128,128]{2,1,0:T(8,128)(2,1)} collective-permute-done((bf16[64,128,128]{2,1,0:T(8,128)(2,1)}, bf16[64,128,128]{2,1,0:T(8,128)(2,1)}, u32[]{:S(2)}, u32[]{:S(2)}) %collective-permute-start.100) | collective-permute-done | bytes 2097184 | tf_op jit(solution)/shard_map/ppermute | solution.py:260
  978.5 10.6 shard_map.113
  991.2 14.4 %collective-permute-done.106.refs_3_ = bf16[64,64,128]{2,1,0:T(8,128)(2,1)} collective-permute-done((bf16[64,64,128]{2,1,0:T(8,128)(2,1)}, bf16[64,64,128]{2,1,0:T(8,128)(2,1)}, u32[]{:S(2)}, u32[]{:S(2)}) %collective-permute-start.106) | collective-permute-done | bytes 1048608 | tf_op jit(solution)/shard_map/ppermute | solution.py:255
  1005.5 20.8 %collective-permute-done.107.refs_4_ = bf16[64,64,128]{2,1,0:T(8,128)(2,1)} collective-permute-done((bf16[64,64,128]{2,1,0:T(8,128)(2,1)}, bf16[64,64,128]{2,1,0:T(8,128)(2,1)}, u32[]{:S(2)}, u32[]{:S(2)}) %collective-permute-start.107) | collective-permute-done | bytes 1048608 | tf_op jit(solution)/shard_map/ppermute | solution.py:255
  1035.4 7.5 shard_map.115
  1042.8 7.5 shard_map.116
  1050.3 7.0 shard_map.117
  1059.4 25.1 %collective-permute-done.108.refs_2_ = bf16[32,128,128]{2,1,0:T(8,128)(2,1)} collective-permute-done((bf16[32,128,128]{2,1,0:T(8,128)(2,1)}, bf16[32,128,128]{2,1,0:T(8,128)(2,1)}, u32[]{:S(2)}, u32[]{:S(2)}) %collective-permute-start.108) | collective-permute-done | bytes 1048608 | tf_op jit(solution)/shard_map/ppermute | solution.py:260
  1135.7 22.1 %collective-permute-done.118.refs_4_ = bf16[64,64,128]{2,1,0:T(8,128)(2,1)} collective-permute-done((bf16[64,64,128]{2,1,0:T(8,128)(2,1)}, bf16[64,64,128]{2,1,0:T(8,128)(2,1)}, u32[]{:S(2)}, u32[]{:S(2)}) %collective-permute-start.118) | collective-permute-done | bytes 1048608 | tf_op jit(solution)/shard_map/ppermute | solution.py:255
  1158.9 7.5 shard_map.122
  1178.5 35.1 %collective-permute-done.127.refs_2_ = bf16[16,128,128]{2,1,0:T(8,128)(2,1)} collective-permute-done((bf16[16,128,128]{2,1,0:T(8,128)(2,1)}, bf16[16,128,128]{2,1,0:T(8,128)(2,1)}, u32[]{:S(2)}, u32[]{:S(2)}) %collective-permute-start.127) | collective-permute-done | bytes 524320 | tf_op jit(solution)/shard_map/ppermute | solution.py:260
  1221.4 7.5 shard_map.126
  1254.8 10.0 collective-permute-done.137.refs_2_
  1286.6 7.8 shard_map.134
  1347.8 7.7 shard_map.142
  (360 shorter events, 495.3 us)
Async XLA Ops:
  107.0 39.4 %collective-permute-start.24 = (bf16[32,64,128]{2,1,0:T(8,128)(2,1)}, bf16[32,64,128]{2,1,0:T(8,128)(2,1)}, u32[]{:S(2)}, u32[]{:S(2)}) collective-permute-start(bf16[32,64,128]{2,1,0:T(8,128)(2,1)} %get-tuple-element.418), channel_id=1, source_target_pairs={{0,3},{1,2},{2,1},{3,0},{4,7},{5,6},{6,5},{7,4}} | collective-permute-start | bytes 1572872 | tf_op jit(solution)/shard_map/ppermute | solution.py:255
  111.5 53.2 %collective-permute-start.25 = (bf16[32,128,128]{2,1,0:T(8,128)(2,1)}, bf16[32,128,128]{2,1,0:T(8,128)(2,1)}, u32[]{:S(2)}, u32[]{:S(2)}) collective-permute-start(bf16[32,128,128]{2,1,0:T(8,128)(2,1)} %get-tuple-element.421), channel_id=1, source_target_pairs={{0,4},{4,0},{1,5},{5,1},{2,6},{6,2},{3,7},{7,3}} | collective-permute-start | bytes 3145736 | tf_op jit(solution)/shard_map/ppermute | solution.py:260
  159.2 44.5 %collective-permute-start.29 = (bf16[64,64,128]{2,1,0:T(8,128)(2,1)}, bf16[64,64,128]{2,1,0:T(8,128)(2,1)}, u32[]{:S(2)}, u32[]{:S(2)}) collective-permute-start(bf16[64,64,128]{2,1,0:T(8,128)(2,1)} %get-tuple-element.429), channel_id=1, source_target_pairs={{0,3},{1,2},{2,1},{3,0},{4,7},{5,6},{6,5},{7,4}} | collective-permute-start | bytes 3145736 | tf_op jit(solution)/shard_map/ppermute | solution.py:255
  164.8 55.3 %collective-permute-start.30 = (bf16[32,128,128]{2,1,0:T(8,128)(2,1)}, bf16[32,128,128]{2,1,0:T(8,128)(2,1)}, u32[]{:S(2)}, u32[]{:S(2)}) collective-permute-start(bf16[32,128,128]{2,1,0:T(8,128)(2,1)} %get-tuple-element.433), channel_id=1, source_target_pairs={{0,4},{4,0},{1,5},{5,1},{2,6},{6,2},{3,7},{7,3}} | collective-permute-start | bytes 3145736 | tf_op jit(solution)/shard_map/ppermute | solution.py:260
  178.2 46.4 %collective-permute-start.31 = (bf16[32,128,128]{2,1,0:T(8,128)(2,1)}, bf16[32,128,128]{2,1,0:T(8,128)(2,1)}, u32[]{:S(2)}, u32[]{:S(2)}) collective-permute-start(bf16[32,128,128]{2,1,0:T(8,128)(2,1)} %get-tuple-element.437), channel_id=1, source_target_pairs={{0,4},{4,0},{1,5},{5,1},{2,6},{6,2},{3,7},{7,3}} | collective-permute-start | bytes 3145736 | tf_op jit(solution)/shard_map/ppermute | solution.py:260
  220.1 71.0 %collective-permute-start.44 = (bf16[64,64,128]{2,1,0:T(8,128)(2,1)}, bf16[64,64,128]{2,1,0:T(8,128)(2,1)}, u32[]{:S(2)}, u32[]{:S(2)}) collective-permute-start(bf16[64,64,128]{2,1,0:T(8,128)(2,1)} %get-tuple-element.459), channel_id=1, source_target_pairs={{0,1},{1,0},{2,3},{3,2},{4,5},{5,4},{6,7},{7,6}} | collective-permute-start | bytes 3145736 | tf_op jit(solution)/shard_map/ppermute | solution.py:255
  220.1 71.0 %collective-permute-start.45 = (bf16[64,64,128]{2,1,0:T(8,128)(2,1)}, bf16[64,64,128]{2,1,0:T(8,128)(2,1)}, u32[]{:S(2)}, u32[]{:S(2)}) collective-permute-start(bf16[64,64,128]{2,1,0:T(8,128)(2,1)} %get-tuple-element.460), channel_id=1, source_target_pairs={{0,2},{1,3},{2,0},{3,1},{4,6},{5,7},{6,4},{7,5}} | collective-permute-start | bytes 3145736 | tf_op jit(solution)/shard_map/ppermute | solution.py:255
  221.8 69.3 %collective-permute-start.46 = (bf16[64,64,128]{2,1,0:T(8,128)(2,1)}, bf16[64,64,128]{2,1,0:T(8,128)(2,1)}, u32[]{:S(2)}, u32[]{:S(2)}) collective-permute-start(bf16[64,64,128]{2,1,0:T(8,128)(2,1)} %get-tuple-element.461), channel_id=1, source_target_pairs={{0,3},{1,2},{2,1},{3,0},{4,7},{5,6},{6,5},{7,4}} | collective-permute-start | bytes 3145736 | tf_op jit(solution)/shard_map/ppermute | solution.py:255
  222.9 77.1 %collective-permute-start.47 = (bf16[64,128,128]{2,1,0:T(8,128)(2,1)}, bf16[64,128,128]{2,1,0:T(8,128)(2,1)}, u32[]{:S(2)}, u32[]{:S(2)}) collective-permute-start(bf16[64,128,128]{2,1,0:T(8,128)(2,1)} %get-tuple-element.464), channel_id=1, source_target_pairs={{0,4},{4,0},{1,5},{5,1},{2,6},{6,2},{3,7},{7,3}} | collective-permute-start | bytes 6291464 | tf_op jit(solution)/shard_map/ppermute | solution.py:260
  224.6 51.8 %collective-permute-start.43 = (bf16[24,64,128]{2,1,0:T(8,128)(2,1)}, bf16[24,64,128]{2,1,0:T(8,128)(2,1)}, u32[]{:S(2)}, u32[]{:S(2)}) collective-permute-start(bf16[24,64,128]{2,1,0:T(8,128)(2,1)} %get-tuple-element.454), channel_id=1, source_target_pairs={{0,3},{1,2},{2,1},{3,0},{4,7},{5,6},{6,5},{7,4}} | collective-permute-start | bytes 1179656 | tf_op jit(solution)/shard_map/ppermute | solution.py:255
  298.0 75.4 %collective-permute-start.49 = (bf16[64,128,128]{2,1,0:T(8,128)(2,1)}, bf16[64,128,128]{2,1,0:T(8,128)(2,1)}, u32[]{:S(2)}, u32[]{:S(2)}) collective-permute-start(bf16[64,128,128]{2,1,0:T(8,128)(2,1)} %get-tuple-element.470), channel_id=1, source_target_pairs={{0,4},{4,0},{1,5},{5,1},{2,6},{6,2},{3,7},{7,3}} | collective-permute-start | bytes 6291464 | tf_op jit(solution)/shard_map/ppermute | solution.py:260
  299.6 69.7 %collective-permute-start.48 = (bf16[32,128,128]{2,1,0:T(8,128)(2,1)}, bf16[32,128,128]{2,1,0:T(8,128)(2,1)}, u32[]{:S(2)}, u32[]{:S(2)}) collective-permute-start(bf16[32,128,128]{2,1,0:T(8,128)(2,1)} %get-tuple-element.467), channel_id=1, source_target_pairs={{0,4},{4,0},{1,5},{5,1},{2,6},{6,2},{3,7},{7,3}} | collective-permute-start | bytes 3145736 | tf_op jit(solution)/shard_map/ppermute | solution.py:260
  310.6 125.0 %collective-permute-start.50 = (bf16[64,128,128]{2,1,0:T(8,128)(2,1)}, bf16[64,128,128]{2,1,0:T(8,128)(2,1)}, u32[]{:S(2)}, u32[]{:S(2)}) collective-permute-start(bf16[64,128,128]{2,1,0:T(8,128)(2,1)} %get-tuple-element.473), channel_id=1, source_target_pairs={{0,4},{4,0},{1,5},{5,1},{2,6},{6,2},{3,7},{7,3}} | collective-permute-start | bytes 6291464 | tf_op jit(solution)/shard_map/ppermute | solution.py:260
  312.2 74.8 %collective-permute-start.51 = (bf16[64,64,128]{2,1,0:T(8,128)(2,1)}, bf16[64,64,128]{2,1,0:T(8,128)(2,1)}, u32[]{:S(2)}, u32[]{:S(2)}) collective-permute-start(bf16[64,64,128]{2,1,0:T(8,128)(2,1)} %get-tuple-element.476), channel_id=1, source_target_pairs={{0,1},{1,0},{2,3},{3,2},{4,5},{5,4},{6,7},{7,6}} | collective-permute-start | bytes 3145736 | tf_op jit(solution)/shard_map/ppermute | solution.py:255
  383.9 84.2 %collective-permute-start.54 = (bf16[64,128,128]{2,1,0:T(8,128)(2,1)}, bf16[64,128,128]{2,1,0:T(8,128)(2,1)}, u32[]{:S(2)}, u32[]{:S(2)}) collective-permute-start(bf16[64,128,128]{2,1,0:T(8,128)(2,1)} %get-tuple-element.481), channel_id=1, source_target_pairs={{0,4},{4,0},{1,5},{5,1},{2,6},{6,2},{3,7},{7,3}} | collective-permute-start | bytes 6291464 | tf_op jit(solution)/shard_map/ppermute | solution.py:260
  387.1 46.3 %collective-permute-start.53 = (bf16[64,64,128]{2,1,0:T(8,128)(2,1)}, bf16[64,64,128]{2,1,0:T(8,128)(2,1)}, u32[]{:S(2)}, u32[]{:S(2)}) collective-permute-start(bf16[64,64,128]{2,1,0:T(8,128)(2,1)} %get-tuple-element.478), channel_id=1, source_target_pairs={{0,3},{1,2},{2,1},{3,0},{4,7},{5,6},{6,5},{7,4}} | collective-permute-start | bytes 3145736 | tf_op jit(solution)/shard_map/ppermute | solution.py:255
  387.1 48.5 %collective-permute-start.55 = (bf16[32,64,128]{2,1,0:T(8,128)(2,1)}, bf16[32,64,128]{2,1,0:T(8,128)(2,1)}, u32[]{:S(2)}, u32[]{:S(2)}) collective-permute-start(bf16[32,64,128]{2,1,0:T(8,128)(2,1)} %get-tuple-element.485), channel_id=1, source_target_pairs={{0,1},{1,0},{2,3},{3,2},{4,5},{5,4},{6,7},{7,6}} | collective-permute-start | bytes 1572872 | tf_op jit(solution)/shard_map/ppermute | solution.py:255
  449.7 95.5 %collective-permute-start.64 = (bf16[64,128,128]{2,1,0:T(8,128)(2,1)}, bf16[64,128,128]{2,1,0:T(8,128)(2,1)}, u32[]{:S(2)}, u32[]{:S(2)}) collective-permute-start(bf16[64,128,128]{2,1,0:T(8,128)(2,1)} %get-tuple-element.500), channel_id=1, source_target_pairs={{0,4},{4,0},{1,5},{5,1},{2,6},{6,2},{3,7},{7,3}} | collective-permute-start | bytes 6291464 | tf_op jit(solution)/shard_map/ppermute | solution.py:260
  455.9 80.4 %collective-permute-start.61 = (bf16[64,64,128]{2,1,0:T(8,128)(2,1)}, bf16[64,64,128]{2,1,0:T(8,128)(2,1)}, u32[]{:S(2)}, u32[]{:S(2)}) collective-permute-start(bf16[64,64,128]{2,1,0:T(8,128)(2,1)} %get-tuple-element.495), channel_id=1, source_target_pairs={{0,1},{1,0},{2,3},{3,2},{4,5},{5,4},{6,7},{7,6}} | collective-permute-start | bytes 3145736 | tf_op jit(solution)/shard_map/ppermute | solution.py:255
  457.0 80.8 %collective-permute-start.62 = (bf16[64,64,128]{2,1,0:T(8,128)(2,1)}, bf16[64,64,128]{2,1,0:T(8,128)(2,1)}, u32[]{:S(2)}, u32[]{:S(2)}) collective-permute-start(bf16[64,64,128]{2,1,0:T(8,128)(2,1)} %get-tuple-element.496), channel_id=1, source_target_pairs={{0,2},{1,3},{2,0},{3,1},{4,6},{5,7},{6,4},{7,5}} | collective-permute-start | bytes 3145736 | tf_op jit(solution)/shard_map/ppermute | solution.py:255
  468.1 69.7 %collective-permute-start.63 = (bf16[64,64,128]{2,1,0:T(8,128)(2,1)}, bf16[64,64,128]{2,1,0:T(8,128)(2,1)}, u32[]{:S(2)}, u32[]{:S(2)}) collective-permute-start(bf16[64,64,128]{2,1,0:T(8,128)(2,1)} %get-tuple-element.497), channel_id=1, source_target_pairs={{0,3},{1,2},{2,1},{3,0},{4,7},{5,6},{6,5},{7,4}} | collective-permute-start | bytes 3145736 | tf_op jit(solution)/shard_map/ppermute | solution.py:255
  468.1 52.8 %collective-permute-start.60 = (bf16[32,64,128]{2,1,0:T(8,128)(2,1)}, bf16[32,64,128]{2,1,0:T(8,128)(2,1)}, u32[]{:S(2)}, u32[]{:S(2)}) collective-permute-start(bf16[32,64,128]{2,1,0:T(8,128)(2,1)} %get-tuple-element.490), channel_id=1, source_target_pairs={{0,3},{1,2},{2,1},{3,0},{4,7},{5,6},{6,5},{7,4}} | collective-permute-start | bytes 1572872 | tf_op jit(solution)/shard_map/ppermute | solution.py:255
  544.7 64.4 %collective-permute-start.68 = (bf16[64,128,128]{2,1,0:T(8,128)(2,1)}, bf16[64,128,128]{2,1,0:T(8,128)(2,1)}, u32[]{:S(2)}, u32[]{:S(2)}) collective-permute-start(bf16[64,128,128]{2,1,0:T(8,128)(2,1)} %get-tuple-element.509), channel_id=1, source_target_pairs={{0,4},{4,0},{1,5},{5,1},{2,6},{6,2},{3,7},{7,3}} | collective-permute-start | bytes 6291464 | tf_op jit(solution)/shard_map/ppermute | solution.py:260
  545.2 38.9 %collective-permute-start.67 = (bf16[64,64,128]{2,1,0:T(8,128)(2,1)}, bf16[64,64,128]{2,1,0:T(8,128)(2,1)}, u32[]{:S(2)}, u32[]{:S(2)}) collective-permute-start(bf16[64,64,128]{2,1,0:T(8,128)(2,1)} %get-tuple-element.505), channel_id=1, source_target_pairs={{0,3},{1,2},{2,1},{3,0},{4,7},{5,6},{6,5},{7,4}} | collective-permute-start | bytes 3145736 | tf_op jit(solution)/shard_map/ppermute | solution.py:255
  555.7 86.2 %collective-permute-start.72 = (bf16[64,128,128]{2,1,0:T(8,128)(2,1)}, bf16[64,128,128]{2,1,0:T(8,128)(2,1)}, u32[]{:S(2)}, u32[]{:S(2)}) collective-permute-start(bf16[64,128,128]{2,1,0:T(8,128)(2,1)} %get-tuple-element.519), channel_id=1, source_target_pairs={{0,4},{4,0},{1,5},{5,1},{2,6},{6,2},{3,7},{7,3}} | collective-permute-start | bytes 6291464 | tf_op jit(solution)/shard_map/ppermute | solution.py:260
  562.6 44.9 %collective-permute-start.70 = (bf16[64,64,128]{2,1,0:T(8,128)(2,1)}, bf16[64,64,128]{2,1,0:T(8,128)(2,1)}, u32[]{:S(2)}, u32[]{:S(2)}) collective-permute-start(bf16[64,64,128]{2,1,0:T(8,128)(2,1)} %get-tuple-element.514), channel_id=1, source_target_pairs={{0,2},{1,3},{2,0},{3,1},{4,6},{5,7},{6,4},{7,5}} | collective-permute-start | bytes 3145736 | tf_op jit(solution)/shard_map/ppermute | solution.py:255
  584.1 49.9 %collective-permute-start.71 = (bf16[64,64,128]{2,1,0:T(8,128)(2,1)}, bf16[64,64,128]{2,1,0:T(8,128)(2,1)}, u32[]{:S(2)}, u32[]{:S(2)}) collective-permute-start(bf16[64,64,128]{2,1,0:T(8,128)(2,1)} %get-tuple-element.515), channel_id=1, source_target_pairs={{0,3},{1,2},{2,1},{3,0},{4,7},{5,6},{6,5},{7,4}} | collective-permute-start | bytes 3145736 | tf_op jit(solution)/shard_map/ppermute | solution.py:255
  586.3 62.4 %collective-permute-start.73 = (bf16[64,64,128]{2,1,0:T(8,128)(2,1)}, bf16[64,64,128]{2,1,0:T(8,128)(2,1)}, u32[]{:S(2)}, u32[]{:S(2)}) collective-permute-start(bf16[64,64,128]{2,1,0:T(8,128)(2,1)} %get-tuple-element.522), channel_id=1, source_target_pairs={{0,1},{1,0},{2,3},{3,2},{4,5},{5,4},{6,7},{7,6}} | collective-permute-start | bytes 3145736 | tf_op jit(solution)/shard_map/ppermute | solution.py:255
  607.5 44.9 %collective-permute-start.74 = (bf16[64,64,128]{2,1,0:T(8,128)(2,1)}, bf16[64,64,128]{2,1,0:T(8,128)(2,1)}, u32[]{:S(2)}, u32[]{:S(2)}) collective-permute-start(bf16[64,64,128]{2,1,0:T(8,128)(2,1)} %get-tuple-element.523), channel_id=1, source_target_pairs={{0,2},{1,3},{2,0},{3,1},{4,6},{5,7},{6,4},{7,5}} | collective-permute-start | bytes 3145736 | tf_op jit(solution)/shard_map/ppermute | solution.py:255
  609.0 64.0 %collective-permute-start.75 = (bf16[64,64,128]{2,1,0:T(8,128)(2,1)}, bf16[64,64,128]{2,1,0:T(8,128)(2,1)}, u32[]{:S(2)}, u32[]{:S(2)}) collective-permute-start(bf16[64,64,128]{2,1,0:T(8,128)(2,1)} %get-tuple-element.524), channel_id=1, source_target_pairs={{0,3},{1,2},{2,1},{3,0},{4,7},{5,6},{6,5},{7,4}} | collective-permute-start | bytes 3145736 | tf_op jit(solution)/shard_map/ppermute | solution.py:255
  634.0 75.1 %collective-permute-start.76 = (bf16[64,128,128]{2,1,0:T(8,128)(2,1)}, bf16[64,128,128]{2,1,0:T(8,128)(2,1)}, u32[]{:S(2)}, u32[]{:S(2)}) collective-permute-start(bf16[64,128,128]{2,1,0:T(8,128)(2,1)} %get-tuple-element.527), channel_id=1, source_target_pairs={{0,4},{4,0},{1,5},{5,1},{2,6},{6,2},{3,7},{7,3}} | collective-permute-start | bytes 6291464 | tf_op jit(solution)/shard_map/ppermute | solution.py:260
  679.9 57.5 %collective-permute-start.80 = (bf16[64,128,128]{2,1,0:T(8,128)(2,1)}, bf16[64,128,128]{2,1,0:T(8,128)(2,1)}, u32[]{:S(2)}, u32[]{:S(2)}) collective-permute-start(bf16[64,128,128]{2,1,0:T(8,128)(2,1)} %get-tuple-element.536), channel_id=1, source_target_pairs={{0,4},{4,0},{1,5},{5,1},{2,6},{6,2},{3,7},{7,3}} | collective-permute-start | bytes 6291464 | tf_op jit(solution)/shard_map/ppermute | solution.py:260
  682.8 46.3 %collective-permute-start.79 = (bf16[64,64,128]{2,1,0:T(8,128)(2,1)}, bf16[64,64,128]{2,1,0:T(8,128)(2,1)}, u32[]{:S(2)}, u32[]{:S(2)}) collective-permute-start(bf16[64,64,128]{2,1,0:T(8,128)(2,1)} %get-tuple-element.533), channel_id=1, source_target_pairs={{0,3},{1,2},{2,1},{3,0},{4,7},{5,6},{6,5},{7,4}} | collective-permute-start | bytes 3145736 | tf_op jit(solution)/shard_map/ppermute | solution.py:255
  683.8 64.8 %collective-permute-start.81 = (bf16[64,64,128]{2,1,0:T(8,128)(2,1)}, bf16[64,64,128]{2,1,0:T(8,128)(2,1)}, u32[]{:S(2)}, u32[]{:S(2)}) collective-permute-start(bf16[64,64,128]{2,1,0:T(8,128)(2,1)} %get-tuple-element.540), channel_id=1, source_target_pairs={{0,1},{1,0},{2,3},{3,2},{4,5},{5,4},{6,7},{7,6}} | collective-permute-start | bytes 3145736 | tf_op jit(solution)/shard_map/ppermute | solution.py:255
  707.5 44.9 %collective-permute-start.82 = (bf16[64,64,128]{2,1,0:T(8,128)(2,1)}, bf16[64,64,128]{2,1,0:T(8,128)(2,1)}, u32[]{:S(2)}, u32[]{:S(2)}) collective-permute-start(bf16[64,64,128]{2,1,0:T(8,128)(2,1)} %get-tuple-element.541), channel_id=1, source_target_pairs={{0,2},{1,3},{2,0},{3,1},{4,6},{5,7},{6,4},{7,5}} | collective-permute-start | bytes 3145736 | tf_op jit(solution)/shard_map/ppermute | solution.py:255
  709.1 64.9 %collective-permute-start.83 = (bf16[64,64,128]{2,1,0:T(8,128)(2,1)}, bf16[64,64,128]{2,1,0:T(8,128)(2,1)}, u32[]{:S(2)}, u32[]{:S(2)}) collective-permute-start(bf16[64,64,128]{2,1,0:T(8,128)(2,1)} %get-tuple-element.542), channel_id=1, source_target_pairs={{0,3},{1,2},{2,1},{3,0},{4,7},{5,6},{6,5},{7,4}} | collective-permute-start | bytes 3145736 | tf_op jit(solution)/shard_map/ppermute | solution.py:255
  735.9 99.6 %collective-permute-start.87 = (bf16[64,128,128]{2,1,0:T(8,128)(2,1)}, bf16[64,128,128]{2,1,0:T(8,128)(2,1)}, u32[]{:S(2)}, u32[]{:S(2)}) collective-permute-start(bf16[64,128,128]{2,1,0:T(8,128)(2,1)} %get-tuple-element.551), channel_id=1, source_target_pairs={{0,4},{4,0},{1,5},{5,1},{2,6},{6,2},{3,7},{7,3}} | collective-permute-start | bytes 6291464 | tf_op jit(solution)/shard_map/ppermute | solution.py:260
  748.0 99.6 %collective-permute-start.88 = (bf16[64,128,128]{2,1,0:T(8,128)(2,1)}, bf16[64,128,128]{2,1,0:T(8,128)(2,1)}, u32[]{:S(2)}, u32[]{:S(2)}) collective-permute-start(bf16[64,128,128]{2,1,0:T(8,128)(2,1)} %get-tuple-element.554), channel_id=1, source_target_pairs={{0,4},{4,0},{1,5},{5,1},{2,6},{6,2},{3,7},{7,3}} | collective-permute-start | bytes 6291464 | tf_op jit(solution)/shard_map/ppermute | solution.py:260
  752.4 44.9 %collective-permute-start.85 = (bf16[64,64,128]{2,1,0:T(8,128)(2,1)}, bf16[64,64,128]{2,1,0:T(8,128)(2,1)}, u32[]{:S(2)}, u32[]{:S(2)}) collective-permute-start(bf16[64,64,128]{2,1,0:T(8,128)(2,1)} %get-tuple-element.547), channel_id=1, source_target_pairs={{0,2},{1,3},{2,0},{3,1},{4,6},{5,7},{6,4},{7,5}} | collective-permute-start | bytes 3145736 | tf_op jit(solution)/shard_map/ppermute | solution.py:255
  774.0 44.9 %collective-permute-start.86 = (bf16[64,64,128]{2,1,0:T(8,128)(2,1)}, bf16[64,64,128]{2,1,0:T(8,128)(2,1)}, u32[]{:S(2)}, u32[]{:S(2)}) collective-permute-start(bf16[64,64,128]{2,1,0:T(8,128)(2,1)} %get-tuple-element.548), channel_id=1, source_target_pairs={{0,3},{1,2},{2,1},{3,0},{4,7},{5,6},{6,5},{7,4}} | collective-permute-start | bytes 3145736 | tf_op jit(solution)/shard_map/ppermute | solution.py:255
  783.0 71.4 %collective-permute-start.89 = (bf16[64,64,128]{2,1,0:T(8,128)(2,1)}, bf16[64,64,128]{2,1,0:T(8,128)(2,1)}, u32[]{:S(2)}, u32[]{:S(2)}) collective-permute-start(bf16[64,64,128]{2,1,0:T(8,128)(2,1)} %get-tuple-element.558), channel_id=1, source_target_pairs={{0,1},{1,0},{2,3},{3,2},{4,5},{5,4},{6,7},{7,6}} | collective-permute-start | bytes 3145736 | tf_op jit(solution)/shard_map/ppermute | solution.py:255
  797.4 57.7 %collective-permute-start.90 = (bf16[64,64,128]{2,1,0:T(8,128)(2,1)}, bf16[64,64,128]{2,1,0:T(8,128)(2,1)}, u32[]{:S(2)}, u32[]{:S(2)}) collective-permute-start(bf16[64,64,128]{2,1,0:T(8,128)(2,1)} %get-tuple-element.559), channel_id=1, source_target_pairs={{0,2},{1,3},{2,0},{3,1},{4,6},{5,7},{6,4},{7,5}} | collective-permute-start | bytes 3145736 | tf_op jit(solution)/shard_map/ppermute | solution.py:255
  819.0 44.9 %collective-permute-start.91 = (bf16[64,64,128]{2,1,0:T(8,128)(2,1)}, bf16[64,64,128]{2,1,0:T(8,128)(2,1)}, u32[]{:S(2)}, u32[]{:S(2)}) collective-permute-start(bf16[64,64,128]{2,1,0:T(8,128)(2,1)} %get-tuple-element.560), channel_id=1, source_target_pairs={{0,3},{1,2},{2,1},{3,0},{4,7},{5,6},{6,5},{7,4}} | collective-permute-start | bytes 3145736 | tf_op jit(solution)/shard_map/ppermute | solution.py:255
  835.5 81.3 %collective-permute-start.95 = (bf16[64,128,128]{2,1,0:T(8,128)(2,1)}, bf16[64,128,128]{2,1,0:T(8,128)(2,1)}, u32[]{:S(2)}, u32[]{:S(2)}) collective-permute-start(bf16[64,128,128]{2,1,0:T(8,128)(2,1)} %get-tuple-element.569), channel_id=1, source_target_pairs={{0,4},{4,0},{1,5},{5,1},{2,6},{6,2},{3,7},{7,3}} | collective-permute-start | bytes 6291464 | tf_op jit(solution)/shard_map/ppermute | solution.py:260
  855.0 52.9 %collective-permute-start.94 = (bf16[64,64,128]{2,1,0:T(8,128)(2,1)}, bf16[64,64,128]{2,1,0:T(8,128)(2,1)}, u32[]{:S(2)}, u32[]{:S(2)}) collective-permute-start(bf16[64,64,128]{2,1,0:T(8,128)(2,1)} %get-tuple-element.565), channel_id=1, source_target_pairs={{0,3},{1,2},{2,1},{3,0},{4,7},{5,6},{6,5},{7,4}} | collective-permute-start | bytes 3145736 | tf_op jit(solution)/shard_map/ppermute | solution.py:255
  863.9 71.8 %collective-permute-start.96 = (bf16[64,128,128]{2,1,0:T(8,128)(2,1)}, bf16[64,128,128]{2,1,0:T(8,128)(2,1)}, u32[]{:S(2)}, u32[]{:S(2)}) collective-permute-start(bf16[64,128,128]{2,1,0:T(8,128)(2,1)} %get-tuple-element.572), channel_id=1, source_target_pairs={{0,4},{4,0},{1,5},{5,1},{2,6},{6,2},{3,7},{7,3}} | collective-permute-start | bytes 6291464 | tf_op jit(solution)/shard_map/ppermute | solution.py:260
  879.1 95.1 %collective-permute-start.100 = (bf16[64,128,128]{2,1,0:T(8,128)(2,1)}, bf16[64,128,128]{2,1,0:T(8,128)(2,1)}, u32[]{:S(2)}, u32[]{:S(2)}) collective-permute-start(bf16[64,128,128]{2,1,0:T(8,128)(2,1)} %get-tuple-element.580), channel_id=1, source_target_pairs={{0,4},{4,0},{1,5},{5,1},{2,6},{6,2},{3,7},{7,3}} | collective-permute-start | bytes 6291464 | tf_op jit(solution)/shard_map/ppermute | solution.py:260
  887.2 41.0 %collective-permute-start.102 = (bf16[64,64,128]{2,1,0:T(8,128)(2,1)}, bf16[64,64,128]{2,1,0:T(8,128)(2,1)}, u32[]{:S(2)}, u32[]{:S(2)}) collective-permute-start(bf16[64,64,128]{2,1,0:T(8,128)(2,1)} %get-tuple-element.586), channel_id=1, source_target_pairs={{0,1},{1,0},{2,3},{3,2},{4,5},{5,4},{6,7},{7,6}} | collective-permute-start | bytes 3145736 | tf_op jit(solution)/shard_map/ppermute | solution.py:255
  928.3 99.7 %collective-permute-start.101 = (bf16[64,128,128]{2,1,0:T(8,128)(2,1)}, bf16[64,128,128]{2,1,0:T(8,128)(2,1)}, u32[]{:S(2)}, u32[]{:S(2)}) collective-permute-start(bf16[64,128,128]{2,1,0:T(8,128)(2,1)} %get-tuple-element.583), channel_id=1, source_target_pairs={{0,4},{4,0},{1,5},{5,1},{2,6},{6,2},{3,7},{7,3}} | collective-permute-start | bytes 6291464 | tf_op jit(solution)/shard_map/ppermute | solution.py:260
  935.7 53.4 %collective-permute-start.104 = (bf16[64,64,128]{2,1,0:T(8,128)(2,1)}, bf16[64,64,128]{2,1,0:T(8,128)(2,1)}, u32[]{:S(2)}, u32[]{:S(2)}) collective-permute-start(bf16[64,64,128]{2,1,0:T(8,128)(2,1)} %get-tuple-element.588), channel_id=1, source_target_pairs={{0,3},{1,2},{2,1},{3,0},{4,7},{5,6},{6,5},{7,4}} | collective-permute-start | bytes 3145736 | tf_op jit(solution)/shard_map/ppermute | solution.py:255
  949.3 41.2 %collective-permute-start.105 = (bf16[64,64,128]{2,1,0:T(8,128)(2,1)}, bf16[64,64,128]{2,1,0:T(8,128)(2,1)}, u32[]{:S(2)}, u32[]{:S(2)}) collective-permute-start(bf16[64,64,128]{2,1,0:T(8,128)(2,1)} %get-tuple-element.592), channel_id=1, source_target_pairs={{0,1},{1,0},{2,3},{3,2},{4,5},{5,4},{6,7},{7,6}} | collective-permute-start | bytes 3145736 | tf_op jit(solution)/shard_map/ppermute | solution.py:255
  959.5 46.0 %collective-permute-start.106 = (bf16[64,64,128]{2,1,0:T(8,128)(2,1)}, bf16[64,64,128]{2,1,0:T(8,128)(2,1)}, u32[]{:S(2)}, u32[]{:S(2)}) collective-permute-start(bf16[64,64,128]{2,1,0:T(8,128)(2,1)} %get-tuple-element.593), channel_id=1, source_target_pairs={{0,2},{1,3},{2,0},{3,1},{4,6},{5,7},{6,4},{7,5}} | collective-permute-start | bytes 3145736 | tf_op jit(solution)/shard_map/ppermute | solution.py:255
  974.3 52.0 %collective-permute-start.107 = (bf16[64,64,128]{2,1,0:T(8,128)(2,1)}, bf16[64,64,128]{2,1,0:T(8,128)(2,1)}, u32[]{:S(2)}, u32[]{:S(2)}) collective-permute-start(bf16[64,64,128]{2,1,0:T(8,128)(2,1)} %get-tuple-element.594), channel_id=1, source_target_pairs={{0,3},{1,2},{2,1},{3,0},{4,7},{5,6},{6,5},{7,4}} | collective-permute-start | bytes 3145736 | tf_op jit(solution)/shard_map/ppermute | solution.py:255
  989.1 131.5 %collective-permute-start.115 = (bf16[64,128,128]{2,1,0:T(8,128)(2,1)}, bf16[64,128,128]{2,1,0:T(8,128)(2,1)}, u32[]{:S(2)}, u32[]{:S(2)}) collective-permute-start(bf16[64,128,128]{2,1,0:T(8,128)(2,1)} %get-tuple-element.612), channel_id=1, source_target_pairs={{0,4},{4,0},{1,5},{5,1},{2,6},{6,2},{3,7},{7,3}} | collective-permute-start | bytes 6291464 | tf_op jit(solution)/shard_map/ppermute | solution.py:260
  990.6 93.9 %collective-permute-start.108 = (bf16[32,128,128]{2,1,0:T(8,128)(2,1)}, bf16[32,128,128]{2,1,0:T(8,128)(2,1)}, u32[]{:S(2)}, u32[]{:S(2)}) collective-permute-start(bf16[32,128,128]{2,1,0:T(8,128)(2,1)} %get-tuple-element.599), channel_id=1, source_target_pairs={{0,4},{4,0},{1,5},{5,1},{2,6},{6,2},{3,7},{7,3}} | collective-permute-start | bytes 3145736 | tf_op jit(solution)/shard_map/ppermute | solution.py:260
  1005.5 51.8 %collective-permute-start.109 = (bf16[32,64,128]{2,1,0:T(8,128)(2,1)}, bf16[32,64,128]{2,1,0:T(8,128)(2,1)}, u32[]{:S(2)}, u32[]{:S(2)}) collective-permute-start(bf16[32,64,128]{2,1,0:T(8,128)(2,1)} %get-tuple-element.602), channel_id=1, source_target_pairs={{0,1},{1,0},{2,3},{3,2},{4,5},{5,4},{6,7},{7,6}} | collective-permute-start | bytes 1572872 | tf_op jit(solution)/shard_map/ppermute | solution.py:255
  1107.6 50.2 %collective-permute-start.118 = (bf16[64,64,128]{2,1,0:T(8,128)(2,1)}, bf16[64,64,128]{2,1,0:T(8,128)(2,1)}, u32[]{:S(2)}, u32[]{:S(2)}) collective-permute-start(bf16[64,64,128]{2,1,0:T(8,128)(2,1)} %get-tuple-element.617), channel_id=1, source_target_pairs={{0,3},{1,2},{2,1},{3,0},{4,7},{5,6},{6,5},{7,4}} | collective-permute-start | bytes 3145736 | tf_op jit(solution)/shard_map/ppermute | solution.py:255
  1119.1 47.3 %collective-permute-start.122 = (bf16[32,128,128]{2,1,0:T(8,128)(2,1)}, bf16[32,128,128]{2,1,0:T(8,128)(2,1)}, u32[]{:S(2)}, u32[]{:S(2)}) collective-permute-start(bf16[32,128,128]{2,1,0:T(8,128)(2,1)} %get-tuple-element.626), channel_id=1, source_target_pairs={{0,4},{4,0},{1,5},{5,1},{2,6},{6,2},{3,7},{7,3}} | collective-permute-start | bytes 3145736 | tf_op jit(solution)/shard_map/ppermute | solution.py:260
  1120.6 57.5 %collective-permute-start.123 = (bf16[32,128,128]{2,1,0:T(8,128)(2,1)}, bf16[32,128,128]{2,1,0:T(8,128)(2,1)}, u32[]{:S(2)}, u32[]{:S(2)}) collective-permute-start(bf16[32,128,128]{2,1,0:T(8,128)(2,1)} %get-tuple-element.629), channel_id=1, source_target_pairs={{0,4},{4,0},{1,5},{5,1},{2,6},{6,2},{3,7},{7,3}} | collective-permute-start | bytes 3145736 | tf_op jit(solution)/shard_map/ppermute | solution.py:260
  1124.3 52.2 %collective-permute-start.129 = (bf16[16,64,128]{2,1,0:T(8,128)(2,1)}, bf16[16,64,128]{2,1,0:T(8,128)(2,1)}, u32[]{:S(2)}, u32[]{:S(2)}) collective-permute-start(bf16[16,64,128]{2,1,0:T(8,128)(2,1)} %get-tuple-element.644), channel_id=1, source_target_pairs={{0,1},{1,0},{2,3},{3,2},{4,5},{5,4},{6,7},{7,6}} | collective-permute-start | bytes 786440 | tf_op jit(solution)/shard_map/ppermute | solution.py:255
  1135.7 78.5 %collective-permute-start.124 = (bf16[64,64,128]{2,1,0:T(8,128)(2,1)}, bf16[64,64,128]{2,1,0:T(8,128)(2,1)}, u32[]{:S(2)}, u32[]{:S(2)}) collective-permute-start(bf16[64,64,128]{2,1,0:T(8,128)(2,1)} %get-tuple-element.632), channel_id=1, source_target_pairs={{0,1},{1,0},{2,3},{3,2},{4,5},{5,4},{6,7},{7,6}} | collective-permute-start | bytes 3145736 | tf_op jit(solution)/shard_map/ppermute | solution.py:255
  1157.8 56.8 %collective-permute-start.125 = (bf16[64,64,128]{2,1,0:T(8,128)(2,1)}, bf16[64,64,128]{2,1,0:T(8,128)(2,1)}, u32[]{:S(2)}, u32[]{:S(2)}) collective-permute-start(bf16[64,64,128]{2,1,0:T(8,128)(2,1)} %get-tuple-element.633), channel_id=1, source_target_pairs={{0,2},{1,3},{2,0},{3,1},{4,6},{5,7},{6,4},{7,5}} | collective-permute-start | bytes 3145736 | tf_op jit(solution)/shard_map/ppermute | solution.py:255
  1166.4 54.2 %collective-permute-start.126 = (bf16[64,64,128]{2,1,0:T(8,128)(2,1)}, bf16[64,64,128]{2,1,0:T(8,128)(2,1)}, u32[]{:S(2)}, u32[]{:S(2)}) collective-permute-start(bf16[64,64,128]{2,1,0:T(8,128)(2,1)} %get-tuple-element.634), channel_id=1, source_target_pairs={{0,3},{1,2},{2,1},{3,0},{4,7},{5,6},{6,5},{7,4}} | collective-permute-start | bytes 3145736 | tf_op jit(solution)/shard_map/ppermute | solution.py:255
  1176.5 52.3 %collective-permute-start.128 = (bf16[32,128,128]{2,1,0:T(8,128)(2,1)}, bf16[32,128,128]{2,1,0:T(8,128)(2,1)}, u32[]{:S(2)}, u32[]{:S(2)}) collective-permute-start(bf16[32,128,128]{2,1,0:T(8,128)(2,1)} %get-tuple-element.641), channel_id=1, source_target_pairs={{0,4},{4,0},{1,5},{5,1},{2,6},{6,2},{3,7},{7,3}} | collective-permute-start | bytes 3145736 | tf_op jit(solution)/shard_map/ppermute | solution.py:260
  (104 other events, 2169.7 us)

commit v2 on v1

--- a/solution.py
+++ b/solution.py
@@ -9,35 +9,22 @@
 BF = jnp.bfloat16
 F32 = jnp.float32
 
-SLABS = (
-    (8, 16, 16, 24,),
-    (32, 32,),
-    (64,),
-    (64,),
-    (64,),
-    (64,),
-    (64,),
-    (64,),
-    (64,),
-    (64,),
-    (32, 32,),
-    (16, 16, 16, 8, 8,),
+SLABS = ((8, 16, 16, 24,), (32, 32,)) + ((64,),) * 8 + ((32, 32,), (16, 16, 16, 8, 8,))
+
+
+ORDER = (
+    1000, 0, 2000, 2001, 3000, 2002, 3001, 1010, 2003, 3002, 2010, 5001, 3003, 5002, 1020, 5000, 2011, 3010,
+    5003, 2020, 1030, 3011, 1040, 5010, 6000, 1050, 2030, 3020, 5011, 3030, 5020, 2040, 5030, 6010, 1060,
+    2050, 3040, 6020, 3050, 1070, 6030, 5040, 2060, 5050, 1080, 2070, 3060, 1090, 6040, 2080, 3070, 5060,
+    1100, 2090, 6060, 3080, 5070, 2100, 3090, 5080, 6050, 6070, 1110, 3100, 2101, 2111, 5090, 6080, 2110,
+    3101, 5100, 6090, 3110, 5101, 2112, 3111, 5110, 2113, 3112, 6100, 5111, 2114, 3113, 5112, 3114, 5113,
+    5114, 6110,
 )
 
 
-ORDER = (
-    (1, 0, (0, 1, 2, 3)), (0, 0, 0), (2, 0, 0), (2, 0, 1), (3, 0, 0), (2, 0, 2), (3, 0, 1), (1, 1, (0, 1)),
-    (2, 0, 3), (3, 0, 2), (2, 1, 0), (5, 0, 1), (3, 0, 3), (5, 0, 2), (1, 2, (0,)), (5, 0, 0), (2, 1, 1),
-    (3, 1, 0), (5, 0, 3), (2, 2, 0), (1, 3, (0,)), (3, 1, 1), (1, 4, (0,)), (5, 1, 0), (6, 0, 0),
-    (1, 5, (0,)), (2, 3, 0), (3, 2, 0), (5, 1, 1), (3, 3, 0), (5, 2, 0), (2, 4, 0), (5, 3, 0), (6, 1, 0),
-    (1, 6, (0,)), (2, 5, 0), (3, 4, 0), (6, 2, 0), (3, 5, 0), (1, 7, (0,)), (6, 3, 0), (5, 4, 0), (2, 6, 0),
-    (5, 5, 0), (1, 8, (0,)), (2, 7, 0), (3, 6, 0), (1, 9, (0,)), (6, 4, 0), (2, 8, 0), (3, 7, 0), (5, 6, 0),
-    (1, 10, (0, 1)), (2, 9, 0), (6, 6, 0), (3, 8, 0), (5, 7, 0), (2, 10, 0), (3, 9, 0), (5, 8, 0), (6, 5, 0),
-    (6, 7, 0), (1, 11, (0, 1, 2, 3, 4)), (3, 10, 0), (2, 10, 1), (2, 11, 1), (5, 9, 0), (6, 8, 0), (2, 11, 0),
-    (3, 10, 1), (5, 10, 0), (6, 9, 0), (3, 11, 0), (5, 10, 1), (2, 11, 2), (3, 11, 1), (5, 11, 0), (2, 11, 3),
-    (3, 11, 2), (6, 10, 0), (5, 11, 1), (2, 11, 4), (3, 11, 3), (5, 11, 2), (3, 11, 4), (5, 11, 3),
-    (5, 11, 4), (6, 11, 0),
-)
+def decode(code):
+    kind, rest = divmod(code, 1000)
+    return kind, *divmod(rest, 10)
 
 
 def dot(a, b):
@@ -266,12 +253,13 @@
         starts = [[sum(cut[:q]) for q in range(len(cut))] for cut in cuts]
         y_in, z_in, j_in, x_in = {}, {}, {}, {}
         w = None
-        for kind, b, q in ORDER:
+        for code in ORDER:
+            kind, b, q = decode(code)
             if kind == 1:
-                parts = [(starts[b][p], cuts[b][p]) for p in q]
+                parts = list(zip(starts[b], cuts[b]))
                 outs, token = stage_one(token, u, a, b, parts, ny, nz)
-                for m, part in enumerate(q):
-                    y_in[b, part] = over_row(outs[4 * m:4 * m + 4], 3 * m)
+                for m in range(len(parts)):
+                    y_in[b, m] = over_row(outs[4 * m:4 * m + 4], 3 * m)
             elif kind == 0:
                 (a6, b4, b5, c_in, c_out), token = prepare(token, a, bm, cm)
             elif kind == 2:

time: 1360 us -> 1360 us (level)
  no operation moved by 1% of the time
where the time goes in v2:
time: 1360 us
  waiting for transfers between devices  697 us (51%)
  Pallas kernels  516 us (38%)
  starting transfers between devices  142 us (10%)
    pallas_call x88, Pallas kernels, call(): pl.pallas_call(wrapped, grid=grid, in_specs=[any_spec()] * lead + list(in...  516 us
    ppermute x126, waiting for transfers between devices, over_row(): got[k] = lax.ppermute(outs[k], 'row', [(r, r ^ k) for r in range(4)])  513 us
    ppermute x42, waiting for transfers between devices, over_col(): return lax.ppermute(value, 'col', [(0, 1), (1, 0)])  184 us
    ppermute x126, starting transfers between devices, over_row(): got[k] = lax.ppermute(outs[k], 'row', [(r, r ^ k) for r in range(4)])  97.1 us
    ppermute x42, starting transfers between devices, over_col(): return lax.ppermute(value, 'col', [(0, 1), (1, 0)])  45.4 us
  transfers between devices with their start and end apart: 168, of which 62 were waited for; matrix products, arithmetic and copies ran while one was open for 0% of the time, Pallas kernels for 37%

profile of v2, /device:TPU:0, one launch (start us, length us, event | category | flops | bytes accessed | tf_op | source)
XLA Modules:
  0.0 1355.7 jit_solution(96637373457025606)
XLA Ops:
  0.0 6.9 shard_map.55
  14.5 12.1 collective-permute-done.1.refs_3_
  37.8 7.1 collective-permute-done.8.refs_3_
  46.4 7.3 collective-permute-done.6.refs_2_
  75.9 16.6 %collective-permute-done.21.refs_2_ = bf16[8,128,128]{2,1,0:T(8,128)(2,1)} collective-permute-done((bf16[8,128,128]{2,1,0:T(8,128)(2,1)}, bf16[8,128,128]{2,1,0:T(8,128)(2,1)}, u32[]{:S(2)}, u32[]{:S(2)}) %collective-permute-start.21) | collective-permute-done | bytes 262176 | tf_op jit(solution)/shard_map/ppermute | solution.py:247
  118.4 10.8 collective-permute-done.20.refs_2_
  185.5 18.2 %collective-permute-done.29.refs_4_ = bf16[64,64,128]{2,1,0:T(8,128)(2,1)} collective-permute-done((bf16[64,64,128]{2,1,0:T(8,128)(2,1)}, bf16[64,64,128]{2,1,0:T(8,128)(2,1)}, u32[]{:S(2)}, u32[]{:S(2)}) %collective-permute-start.29) | collective-permute-done | bytes 1048608 | tf_op jit(solution)/shard_map/ppermute | solution.py:242
  205.9 6.9 shard_map.74
  213.2 6.9 shard_map.75
  242.1 34.3 %collective-permute-done.43.refs_16_ = bf16[24,64,128]{2,1,0:T(8,128)(2,1)} collective-permute-done((bf16[24,64,128]{2,1,0:T(8,128)(2,1)}, bf16[24,64,128]{2,1,0:T(8,128)(2,1)}, u32[]{:S(2)}, u32[]{:S(2)}) %collective-permute-start.43) | collective-permute-done | bytes 393248 | tf_op jit(solution)/shard_map/ppermute | solution.py:242
  276.4 7.9 shard_map.79
  284.3 6.8 shard_map.80
  291.1 6.9 shard_map.81
  300.0 10.6 shard_map.82
  312.2 57.0 %collective-permute-done.48.refs_2_ = bf16[32,128,128]{2,1,0:T(8,128)(2,1)} collective-permute-done((bf16[32,128,128]{2,1,0:T(8,128)(2,1)}, bf16[32,128,128]{2,1,0:T(8,128)(2,1)}, u32[]{:S(2)}, u32[]{:S(2)}) %collective-permute-start.48) | collective-permute-done | bytes 1048608 | tf_op jit(solution)/shard_map/ppermute | solution.py:247
  373.4 10.6 shard_map.84
  387.7 24.2 %collective-permute-done.52.refs_3_ = bf16[64,64,128]{2,1,0:T(8,128)(2,1)} collective-permute-done((bf16[64,64,128]{2,1,0:T(8,128)(2,1)}, bf16[64,64,128]{2,1,0:T(8,128)(2,1)}, u32[]{:S(2)}, u32[]{:S(2)}) %collective-permute-start.52) | collective-permute-done | bytes 1048608 | tf_op jit(solution)/shard_map/ppermute | solution.py:242
  413.4 20.0 %collective-permute-done.53.refs_4_ = bf16[64,64,128]{2,1,0:T(8,128)(2,1)} collective-permute-done((bf16[64,64,128]{2,1,0:T(8,128)(2,1)}, bf16[64,64,128]{2,1,0:T(8,128)(2,1)}, u32[]{:S(2)}, u32[]{:S(2)}) %collective-permute-start.53) | collective-permute-done | bytes 1048608 | tf_op jit(solution)/shard_map/ppermute | solution.py:242
  442.8 6.9 shard_map.86
  458.5 9.6 collective-permute-done.58.refs_6_
  476.5 44.3 %collective-permute-done.60.refs_8_ = bf16[32,64,128]{2,1,0:T(8,128)(2,1)} collective-permute-done((bf16[32,64,128]{2,1,0:T(8,128)(2,1)}, bf16[32,64,128]{2,1,0:T(8,128)(2,1)}, u32[]{:S(2)}, u32[]{:S(2)}) %collective-permute-start.60) | collective-permute-done | bytes 524320 | tf_op jit(solution)/shard_map/ppermute | solution.py:242
  521.6 7.8 shard_map.88
  529.4 6.8 shard_map.89
  537.8 6.9 shard_map.90
  545.2 10.5 shard_map.91
  564.1 20.0 %collective-permute-done.67.refs_4_ = bf16[64,64,128]{2,1,0:T(8,128)(2,1)} collective-permute-done((bf16[64,64,128]{2,1,0:T(8,128)(2,1)}, bf16[64,64,128]{2,1,0:T(8,128)(2,1)}, u32[]{:S(2)}, u32[]{:S(2)}) %collective-permute-start.67) | collective-permute-done | bytes 1048608 | tf_op jit(solution)/shard_map/ppermute | solution.py:242
  586.3 21.2 %collective-permute-done.70.refs_3_ = bf16[64,64,128]{2,1,0:T(8,128)(2,1)} collective-permute-done((bf16[64,64,128]{2,1,0:T(8,128)(2,1)}, bf16[64,64,128]{2,1,0:T(8,128)(2,1)}, u32[]{:S(2)}, u32[]{:S(2)}) %collective-permute-start.70) | collective-permute-done | bytes 1048608 | tf_op jit(solution)/shard_map/ppermute | solution.py:242
  609.0 7.5 shard_map.92
  616.5 10.6 shard_map.93
  634.5 7.5 shard_map.95
  652.5 20.6 %collective-permute-done.75.refs_4_ = bf16[64,64,128]{2,1,0:T(8,128)(2,1)} collective-permute-done((bf16[64,64,128]{2,1,0:T(8,128)(2,1)}, bf16[64,64,128]{2,1,0:T(8,128)(2,1)}, u32[]{:S(2)}, u32[]{:S(2)}) %collective-permute-start.75) | collective-permute-done | bytes 1048608 | tf_op jit(solution)/shard_map/ppermute | solution.py:242
  673.1 6.9 shard_map.97
  684.1 23.3 %collective-permute-done.78.refs_3_ = bf16[64,64,128]{2,1,0:T(8,128)(2,1)} collective-permute-done((bf16[64,64,128]{2,1,0:T(8,128)(2,1)}, bf16[64,64,128]{2,1,0:T(8,128)(2,1)}, u32[]{:S(2)}, u32[]{:S(2)}) %collective-permute-start.78) | collective-permute-done | bytes 1048608 | tf_op jit(solution)/shard_map/ppermute | solution.py:242
  729.1 6.8 shard_map.100
  737.4 10.6 shard_map.101
  754.0 20.0 %collective-permute-done.83.refs_4_ = bf16[64,64,128]{2,1,0:T(8,128)(2,1)} collective-permute-done((bf16[64,64,128]{2,1,0:T(8,128)(2,1)}, bf16[64,64,128]{2,1,0:T(8,128)(2,1)}, u32[]{:S(2)}, u32[]{:S(2)}) %collective-permute-start.83) | collective-permute-done | bytes 1048608 | tf_op jit(solution)/shard_map/ppermute | solution.py:242
  783.0 14.3 %collective-permute-done.85.refs_3_ = bf16[64,64,128]{2,1,0:T(8,128)(2,1)} collective-permute-done((bf16[64,64,128]{2,1,0:T(8,128)(2,1)}, bf16[64,64,128]{2,1,0:T(8,128)(2,1)}, u32[]{:S(2)}, u32[]{:S(2)}) %collective-permute-start.85) | collective-permute-done | bytes 1048608 | tf_op jit(solution)/shard_map/ppermute | solution.py:242
  799.0 20.0 %collective-permute-done.86.refs_4_ = bf16[64,64,128]{2,1,0:T(8,128)(2,1)} collective-permute-done((bf16[64,64,128]{2,1,0:T(8,128)(2,1)}, bf16[64,64,128]{2,1,0:T(8,128)(2,1)}, u32[]{:S(2)}, u32[]{:S(2)}) %collective-permute-start.86) | collective-permute-done | bytes 1048608 | tf_op jit(solution)/shard_map/ppermute | solution.py:242
  821.2 7.5 shard_map.103
  828.6 6.9 shard_map.104
  837.1 10.6 shard_map.105
  856.3 7.6 collective-permute-done.91.refs_4_
  865.4 6.9 shard_map.107
  872.3 6.8 shard_map.108
  879.7 7.6 collective-permute-done.93.refs_3_
  887.2 20.6 %collective-permute-done.94.refs_4_ = bf16[64,64,128]{2,1,0:T(8,128)(2,1)} collective-permute-done((bf16[64,64,128]{2,1,0:T(8,128)(2,1)}, bf16[64,64,128]{2,1,0:T(8,128)(2,1)}, u32[]{:S(2)}, u32[]{:S(2)}) %collective-permute-start.94) | collective-permute-done | bytes 1048608 | tf_op jit(solution)/shard_map/ppermute | solution.py:242
  909.4 7.5 shard_map.109
  917.7 10.6 shard_map.110
  949.4 10.1 collective-permute-done.99.refs_4_
  960.5 13.8 %collective-permute-done.100.refs_2_ = bf16[64,128,128]{2,1,0:T(8,128)(2,1)} collective-permute-done((bf16[64,128,128]{2,1,0:T(8,128)(2,1)}, bf16[64,128,128]{2,1,0:T(8,128)(2,1)}, u32[]{:S(2)}, u32[]{:S(2)}) %collective-permute-start.100) | collective-permute-done | bytes 2097184 | tf_op jit(solution)/shard_map/ppermute | solution.py:247
  978.5 10.6 shard_map.113
  991.2 14.4 %collective-permute-done.106.refs_3_ = bf16[64,64,128]{2,1,0:T(8,128)(2,1)} collective-permute-done((bf16[64,64,128]{2,1,0:T(8,128)(2,1)}, bf16[64,64,128]{2,1,0:T(8,128)(2,1)}, u32[]{:S(2)}, u32[]{:S(2)}) %collective-permute-start.106) | collective-permute-done | bytes 1048608 | tf_op jit(solution)/shard_map/ppermute | solution.py:242
  1005.5 20.8 %collective-permute-done.107.refs_4_ = bf16[64,64,128]{2,1,0:T(8,128)(2,1)} collective-permute-done((bf16[64,64,128]{2,1,0:T(8,128)(2,1)}, bf16[64,64,128]{2,1,0:T(8,128)(2,1)}, u32[]{:S(2)}, u32[]{:S(2)}) %collective-permute-start.107) | collective-permute-done | bytes 1048608 | tf_op jit(solution)/shard_map/ppermute | solution.py:242
  1035.4 7.5 shard_map.115
  1042.8 7.5 shard_map.116
  1050.3 7.0 shard_map.117
  1059.4 25.1 %collective-permute-done.108.refs_2_ = bf16[32,128,128]{2,1,0:T(8,128)(2,1)} collective-permute-done((bf16[32,128,128]{2,1,0:T(8,128)(2,1)}, bf16[32,128,128]{2,1,0:T(8,128)(2,1)}, u32[]{:S(2)}, u32[]{:S(2)}) %collective-permute-start.108) | collective-permute-done | bytes 1048608 | tf_op jit(solution)/shard_map/ppermute | solution.py:247
  1135.7 22.1 %collective-permute-done.118.refs_4_ = bf16[64,64,128]{2,1,0:T(8,128)(2,1)} collective-permute-done((bf16[64,64,128]{2,1,0:T(8,128)(2,1)}, bf16[64,64,128]{2,1,0:T(8,128)(2,1)}, u32[]{:S(2)}, u32[]{:S(2)}) %collective-permute-start.118) | collective-permute-done | bytes 1048608 | tf_op jit(solution)/shard_map/ppermute | solution.py:242
  1158.9 7.5 shard_map.122
  1178.5 35.1 %collective-permute-done.127.refs_2_ = bf16[16,128,128]{2,1,0:T(8,128)(2,1)} collective-permute-done((bf16[16,128,128]{2,1,0:T(8,128)(2,1)}, bf16[16,128,128]{2,1,0:T(8,128)(2,1)}, u32[]{:S(2)}, u32[]{:S(2)}) %collective-permute-start.127) | collective-permute-done | bytes 524320 | tf_op jit(solution)/shard_map/ppermute | solution.py:247
  1221.4 7.5 shard_map.126
  1254.8 10.0 collective-permute-done.137.refs_2_
  1286.6 7.8 shard_map.134
  1347.8 7.7 shard_map.142
  (360 shorter events, 495.3 us)
Async XLA Ops:
  107.0 39.4 %collective-permute-start.24 = (bf16[32,64,128]{2,1,0:T(8,128)(2,1)}, bf16[32,64,128]{2,1,0:T(8,128)(2,1)}, u32[]{:S(2)}, u32[]{:S(2)}) collective-permute-start(bf16[32,64,128]{2,1,0:T(8,128)(2,1)} %get-tuple-element.418), channel_id=1, source_target_pairs={{0,3},{1,2},{2,1},{3,0},{4,7},{5,6},{6,5},{7,4}} | collective-permute-start | bytes 1572872 | tf_op jit(solution)/shard_map/ppermute | solution.py:242
  111.5 53.2 %collective-permute-start.25 = (bf16[32,128,128]{2,1,0:T(8,128)(2,1)}, bf16[32,128,128]{2,1,0:T(8,128)(2,1)}, u32[]{:S(2)}, u32[]{:S(2)}) collective-permute-start(bf16[32,128,128]{2,1,0:T(8,128)(2,1)} %get-tuple-element.421), channel_id=1, source_target_pairs={{0,4},{4,0},{1,5},{5,1},{2,6},{6,2},{3,7},{7,3}} | collective-permute-start | bytes 3145736 | tf_op jit(solution)/shard_map/ppermute | solution.py:247
  159.2 44.5 %collective-permute-start.29 = (bf16[64,64,128]{2,1,0:T(8,128)(2,1)}, bf16[64,64,128]{2,1,0:T(8,128)(2,1)}, u32[]{:S(2)}, u32[]{:S(2)}) collective-permute-start(bf16[64,64,128]{2,1,0:T(8,128)(2,1)} %get-tuple-element.429), channel_id=1, source_target_pairs={{0,3},{1,2},{2,1},{3,0},{4,7},{5,6},{6,5},{7,4}} | collective-permute-start | bytes 3145736 | tf_op jit(solution)/shard_map/ppermute | solution.py:242
  164.8 55.3 %collective-permute-start.30 = (bf16[32,128,128]{2,1,0:T(8,128)(2,1)}, bf16[32,128,128]{2,1,0:T(8,128)(2,1)}, u32[]{:S(2)}, u32[]{:S(2)}) collective-permute-start(bf16[32,128,128]{2,1,0:T(8,128)(2,1)} %get-tuple-element.433), channel_id=1, source_target_pairs={{0,4},{4,0},{1,5},{5,1},{2,6},{6,2},{3,7},{7,3}} | collective-permute-start | bytes 3145736 | tf_op jit(solution)/shard_map/ppermute | solution.py:247
  178.2 46.4 %collective-permute-start.31 = (bf16[32,128,128]{2,1,0:T(8,128)(2,1)}, bf16[32,128,128]{2,1,0:T(8,128)(2,1)}, u32[]{:S(2)}, u32[]{:S(2)}) collective-permute-start(bf16[32,128,128]{2,1,0:T(8,128)(2,1)} %get-tuple-element.437), channel_id=1, source_target_pairs={{0,4},{4,0},{1,5},{5,1},{2,6},{6,2},{3,7},{7,3}} | collective-permute-start | bytes 3145736 | tf_op jit(solution)/shard_map/ppermute | solution.py:247
  220.1 71.0 %collective-permute-start.44 = (bf16[64,64,128]{2,1,0:T(8,128)(2,1)}, bf16[64,64,128]{2,1,0:T(8,128)(2,1)}, u32[]{:S(2)}, u32[]{:S(2)}) collective-permute-start(bf16[64,64,128]{2,1,0:T(8,128)(2,1)} %get-tuple-element.459), channel_id=1, source_target_pairs={{0,1},{1,0},{2,3},{3,2},{4,5},{5,4},{6,7},{7,6}} | collective-permute-start | bytes 3145736 | tf_op jit(solution)/shard_map/ppermute | solution.py:242
  220.1 71.0 %collective-permute-start.45 = (bf16[64,64,128]{2,1,0:T(8,128)(2,1)}, bf16[64,64,128]{2,1,0:T(8,128)(2,1)}, u32[]{:S(2)}, u32[]{:S(2)}) collective-permute-start(bf16[64,64,128]{2,1,0:T(8,128)(2,1)} %get-tuple-element.460), channel_id=1, source_target_pairs={{0,2},{1,3},{2,0},{3,1},{4,6},{5,7},{6,4},{7,5}} | collective-permute-start | bytes 3145736 | tf_op jit(solution)/shard_map/ppermute | solution.py:242
  221.8 69.3 %collective-permute-start.46 = (bf16[64,64,128]{2,1,0:T(8,128)(2,1)}, bf16[64,64,128]{2,1,0:T(8,128)(2,1)}, u32[]{:S(2)}, u32[]{:S(2)}) collective-permute-start(bf16[64,64,128]{2,1,0:T(8,128)(2,1)} %get-tuple-element.461), channel_id=1, source_target_pairs={{0,3},{1,2},{2,1},{3,0},{4,7},{5,6},{6,5},{7,4}} | collective-permute-start | bytes 3145736 | tf_op jit(solution)/shard_map/ppermute | solution.py:242
  222.9 77.1 %collective-permute-start.47 = (bf16[64,128,128]{2,1,0:T(8,128)(2,1)}, bf16[64,128,128]{2,1,0:T(8,128)(2,1)}, u32[]{:S(2)}, u32[]{:S(2)}) collective-permute-start(bf16[64,128,128]{2,1,0:T(8,128)(2,1)} %get-tuple-element.464), channel_id=1, source_target_pairs={{0,4},{4,0},{1,5},{5,1},{2,6},{6,2},{3,7},{7,3}} | collective-permute-start | bytes 6291464 | tf_op jit(solution)/shard_map/ppermute | solution.py:247
  224.6 51.8 %collective-permute-start.43 = (bf16[24,64,128]{2,1,0:T(8,128)(2,1)}, bf16[24,64,128]{2,1,0:T(8,128)(2,1)}, u32[]{:S(2)}, u32[]{:S(2)}) collective-permute-start(bf16[24,64,128]{2,1,0:T(8,128)(2,1)} %get-tuple-element.454), channel_id=1, source_target_pairs={{0,3},{1,2},{2,1},{3,0},{4,7},{5,6},{6,5},{7,4}} | collective-permute-start | bytes 1179656 | tf_op jit(solution)/shard_map/ppermute | solution.py:242
  298.0 75.4 %collective-permute-start.49 = (bf16[64,128,128]{2,1,0:T(8,128)(2,1)}, bf16[64,128,128]{2,1,0:T(8,128)(2,1)}, u32[]{:S(2)}, u32[]{:S(2)}) collective-permute-start(bf16[64,128,128]{2,1,0:T(8,128)(2,1)} %get-tuple-element.470), channel_id=1, source_target_pairs={{0,4},{4,0},{1,5},{5,1},{2,6},{6,2},{3,7},{7,3}} | collective-permute-start | bytes 6291464 | tf_op jit(solution)/shard_map/ppermute | solution.py:247
  299.6 69.7 %collective-permute-start.48 = (bf16[32,128,128]{2,1,0:T(8,128)(2,1)}, bf16[32,128,128]{2,1,0:T(8,128)(2,1)}, u32[]{:S(2)}, u32[]{:S(2)}) collective-permute-start(bf16[32,128,128]{2,1,0:T(8,128)(2,1)} %get-tuple-element.467), channel_id=1, source_target_pairs={{0,4},{4,0},{1,5},{5,1},{2,6},{6,2},{3,7},{7,3}} | collective-permute-start | bytes 3145736 | tf_op jit(solution)/shard_map/ppermute | solution.py:247
  310.6 125.0 %collective-permute-start.50 = (bf16[64,128,128]{2,1,0:T(8,128)(2,1)}, bf16[64,128,128]{2,1,0:T(8,128)(2,1)}, u32[]{:S(2)}, u32[]{:S(2)}) collective-permute-start(bf16[64,128,128]{2,1,0:T(8,128)(2,1)} %get-tuple-element.473), channel_id=1, source_target_pairs={{0,4},{4,0},{1,5},{5,1},{2,6},{6,2},{3,7},{7,3}} | collective-permute-start | bytes 6291464 | tf_op jit(solution)/shard_map/ppermute | solution.py:247
  312.2 74.8 %collective-permute-start.51 = (bf16[64,64,128]{2,1,0:T(8,128)(2,1)}, bf16[64,64,128]{2,1,0:T(8,128)(2,1)}, u32[]{:S(2)}, u32[]{:S(2)}) collective-permute-start(bf16[64,64,128]{2,1,0:T(8,128)(2,1)} %get-tuple-element.476), channel_id=1, source_target_pairs={{0,1},{1,0},{2,3},{3,2},{4,5},{5,4},{6,7},{7,6}} | collective-permute-start | bytes 3145736 | tf_op jit(solution)/shard_map/ppermute | solution.py:242
  383.9 84.2 %collective-permute-start.54 = (bf16[64,128,128]{2,1,0:T(8,128)(2,1)}, bf16[64,128,128]{2,1,0:T(8,128)(2,1)}, u32[]{:S(2)}, u32[]{:S(2)}) collective-permute-start(bf16[64,128,128]{2,1,0:T(8,128)(2,1)} %get-tuple-element.481), channel_id=1, source_target_pairs={{0,4},{4,0},{1,5},{5,1},{2,6},{6,2},{3,7},{7,3}} | collective-permute-start | bytes 6291464 | tf_op jit(solution)/shard_map/ppermute | solution.py:247
  387.1 46.3 %collective-permute-start.53 = (bf16[64,64,128]{2,1,0:T(8,128)(2,1)}, bf16[64,64,128]{2,1,0:T(8,128)(2,1)}, u32[]{:S(2)}, u32[]{:S(2)}) collective-permute-start(bf16[64,64,128]{2,1,0:T(8,128)(2,1)} %get-tuple-element.478), channel_id=1, source_target_pairs={{0,3},{1,2},{2,1},{3,0},{4,7},{5,6},{6,5},{7,4}} | collective-permute-start | bytes 3145736 | tf_op jit(solution)/shard_map/ppermute | solution.py:242
  387.1 48.5 %collective-permute-start.55 = (bf16[32,64,128]{2,1,0:T(8,128)(2,1)}, bf16[32,64,128]{2,1,0:T(8,128)(2,1)}, u32[]{:S(2)}, u32[]{:S(2)}) collective-permute-start(bf16[32,64,128]{2,1,0:T(8,128)(2,1)} %get-tuple-element.485), channel_id=1, source_target_pairs={{0,1},{1,0},{2,3},{3,2},{4,5},{5,4},{6,7},{7,6}} | collective-permute-start | bytes 1572872 | tf_op jit(solution)/shard_map/ppermute | solution.py:242
  449.7 95.5 %collective-permute-start.64 = (bf16[64,128,128]{2,1,0:T(8,128)(2,1)}, bf16[64,128,128]{2,1,0:T(8,128)(2,1)}, u32[]{:S(2)}, u32[]{:S(2)}) collective-permute-start(bf16[64,128,128]{2,1,0:T(8,128)(2,1)} %get-tuple-element.500), channel_id=1, source_target_pairs={{0,4},{4,0},{1,5},{5,1},{2,6},{6,2},{3,7},{7,3}} | collective-permute-start | bytes 6291464 | tf_op jit(solution)/shard_map/ppermute | solution.py:247
  455.9 80.4 %collective-permute-start.61 = (bf16[64,64,128]{2,1,0:T(8,128)(2,1)}, bf16[64,64,128]{2,1,0:T(8,128)(2,1)}, u32[]{:S(2)}, u32[]{:S(2)}) collective-permute-start(bf16[64,64,128]{2,1,0:T(8,128)(2,1)} %get-tuple-element.495), channel_id=1, source_target_pairs={{0,1},{1,0},{2,3},{3,2},{4,5},{5,4},{6,7},{7,6}} | collective-permute-start | bytes 3145736 | tf_op jit(solution)/shard_map/ppermute | solution.py:242
  457.0 80.8 %collective-permute-start.62 = (bf16[64,64,128]{2,1,0:T(8,128)(2,1)}, bf16[64,64,128]{2,1,0:T(8,128)(2,1)}, u32[]{:S(2)}, u32[]{:S(2)}) collective-permute-start(bf16[64,64,128]{2,1,0:T(8,128)(2,1)} %get-tuple-element.496), channel_id=1, source_target_pairs={{0,2},{1,3},{2,0},{3,1},{4,6},{5,7},{6,4},{7,5}} | collective-permute-start | bytes 3145736 | tf_op jit(solution)/shard_map/ppermute | solution.py:242
  468.1 69.7 %collective-permute-start.63 = (bf16[64,64,128]{2,1,0:T(8,128)(2,1)}, bf16[64,64,128]{2,1,0:T(8,128)(2,1)}, u32[]{:S(2)}, u32[]{:S(2)}) collective-permute-start(bf16[64,64,128]{2,1,0:T(8,128)(2,1)} %get-tuple-element.497), channel_id=1, source_target_pairs={{0,3},{1,2},{2,1},{3,0},{4,7},{5,6},{6,5},{7,4}} | collective-permute-start | bytes 3145736 | tf_op jit(solution)/shard_map/ppermute | solution.py:242
  468.1 52.8 %collective-permute-start.60 = (bf16[32,64,128]{2,1,0:T(8,128)(2,1)}, bf16[32,64,128]{2,1,0:T(8,128)(2,1)}, u32[]{:S(2)}, u32[]{:S(2)}) collective-permute-start(bf16[32,64,128]{2,1,0:T(8,128)(2,1)} %get-tuple-element.490), channel_id=1, source_target_pairs={{0,3},{1,2},{2,1},{3,0},{4,7},{5,6},{6,5},{7,4}} | collective-permute-start | bytes 1572872 | tf_op jit(solution)/shard_map/ppermute | solution.py:242
  544.7 64.4 %collective-permute-start.68 = (bf16[64,128,128]{2,1,0:T(8,128)(2,1)}, bf16[64,128,128]{2,1,0:T(8,128)(2,1)}, u32[]{:S(2)}, u32[]{:S(2)}) collective-permute-start(bf16[64,128,128]{2,1,0:T(8,128)(2,1)} %get-tuple-element.509), channel_id=1, source_target_pairs={{0,4},{4,0},{1,5},{5,1},{2,6},{6,2},{3,7},{7,3}} | collective-permute-start | bytes 6291464 | tf_op jit(solution)/shard_map/ppermute | solution.py:247
  545.2 38.9 %collective-permute-start.67 = (bf16[64,64,128]{2,1,0:T(8,128)(2,1)}, bf16[64,64,128]{2,1,0:T(8,128)(2,1)}, u32[]{:S(2)}, u32[]{:S(2)}) collective-permute-start(bf16[64,64,128]{2,1,0:T(8,128)(2,1)} %get-tuple-element.505), channel_id=1, source_target_pairs={{0,3},{1,2},{2,1},{3,0},{4,7},{5,6},{6,5},{7,4}} | collective-permute-start | bytes 3145736 | tf_op jit(solution)/shard_map/ppermute | solution.py:242
  555.7 86.2 %collective-permute-start.72 = (bf16[64,128,128]{2,1,0:T(8,128)(2,1)}, bf16[64,128,128]{2,1,0:T(8,128)(2,1)}, u32[]{:S(2)}, u32[]{:S(2)}) collective-permute-start(bf16[64,128,128]{2,1,0:T(8,128)(2,1)} %get-tuple-element.519), channel_id=1, source_target_pairs={{0,4},{4,0},{1,5},{5,1},{2,6},{6,2},{3,7},{7,3}} | collective-permute-start | bytes 6291464 | tf_op jit(solution)/shard_map/ppermute | solution.py:247
  562.6 44.9 %collective-permute-start.70 = (bf16[64,64,128]{2,1,0:T(8,128)(2,1)}, bf16[64,64,128]{2,1,0:T(8,128)(2,1)}, u32[]{:S(2)}, u32[]{:S(2)}) collective-permute-start(bf16[64,64,128]{2,1,0:T(8,128)(2,1)} %get-tuple-element.514), channel_id=1, source_target_pairs={{0,2},{1,3},{2,0},{3,1},{4,6},{5,7},{6,4},{7,5}} | collective-permute-start | bytes 3145736 | tf_op jit(solution)/shard_map/ppermute | solution.py:242
  584.1 49.9 %collective-permute-start.71 = (bf16[64,64,128]{2,1,0:T(8,128)(2,1)}, bf16[64,64,128]{2,1,0:T(8,128)(2,1)}, u32[]{:S(2)}, u32[]{:S(2)}) collective-permute-start(bf16[64,64,128]{2,1,0:T(8,128)(2,1)} %get-tuple-element.515), channel_id=1, source_target_pairs={{0,3},{1,2},{2,1},{3,0},{4,7},{5,6},{6,5},{7,4}} | collective-permute-start | bytes 3145736 | tf_op jit(solution)/shard_map/ppermute | solution.py:242
  586.3 62.4 %collective-permute-start.73 = (bf16[64,64,128]{2,1,0:T(8,128)(2,1)}, bf16[64,64,128]{2,1,0:T(8,128)(2,1)}, u32[]{:S(2)}, u32[]{:S(2)}) collective-permute-start(bf16[64,64,128]{2,1,0:T(8,128)(2,1)} %get-tuple-element.522), channel_id=1, source_target_pairs={{0,1},{1,0},{2,3},{3,2},{4,5},{5,4},{6,7},{7,6}} | collective-permute-start | bytes 3145736 | tf_op jit(solution)/shard_map/ppermute | solution.py:242
  607.5 44.9 %collective-permute-start.74 = (bf16[64,64,128]{2,1,0:T(8,128)(2,1)}, bf16[64,64,128]{2,1,0:T(8,128)(2,1)}, u32[]{:S(2)}, u32[]{:S(2)}) collective-permute-start(bf16[64,64,128]{2,1,0:T(8,128)(2,1)} %get-tuple-element.523), channel_id=1, source_target_pairs={{0,2},{1,3},{2,0},{3,1},{4,6},{5,7},{6,4},{7,5}} | collective-permute-start | bytes 3145736 | tf_op jit(solution)/shard_map/ppermute | solution.py:242
  609.0 64.0 %collective-permute-start.75 = (bf16[64,64,128]{2,1,0:T(8,128)(2,1)}, bf16[64,64,128]{2,1,0:T(8,128)(2,1)}, u32[]{:S(2)}, u32[]{:S(2)}) collective-permute-start(bf16[64,64,128]{2,1,0:T(8,128)(2,1)} %get-tuple-element.524), channel_id=1, source_target_pairs={{0,3},{1,2},{2,1},{3,0},{4,7},{5,6},{6,5},{7,4}} | collective-permute-start | bytes 3145736 | tf_op jit(solution)/shard_map/ppermute | solution.py:242
  634.0 75.1 %collective-permute-start.76 = (bf16[64,128,128]{2,1,0:T(8,128)(2,1)}, bf16[64,128,128]{2,1,0:T(8,128)(2,1)}, u32[]{:S(2)}, u32[]{:S(2)}) collective-permute-start(bf16[64,128,128]{2,1,0:T(8,128)(2,1)} %get-tuple-element.527), channel_id=1, source_target_pairs={{0,4},{4,0},{1,5},{5,1},{2,6},{6,2},{3,7},{7,3}} | collective-permute-start | bytes 6291464 | tf_op jit(solution)/shard_map/ppermute | solution.py:247
  679.9 57.5 %collective-permute-start.80 = (bf16[64,128,128]{2,1,0:T(8,128)(2,1)}, bf16[64,128,128]{2,1,0:T(8,128)(2,1)}, u32[]{:S(2)}, u32[]{:S(2)}) collective-permute-start(bf16[64,128,128]{2,1,0:T(8,128)(2,1)} %get-tuple-element.536), channel_id=1, source_target_pairs={{0,4},{4,0},{1,5},{5,1},{2,6},{6,2},{3,7},{7,3}} | collective-permute-start | bytes 6291464 | tf_op jit(solution)/shard_map/ppermute | solution.py:247
  682.8 46.3 %collective-permute-start.79 = (bf16[64,64,128]{2,1,0:T(8,128)(2,1)}, bf16[64,64,128]{2,1,0:T(8,128)(2,1)}, u32[]{:S(2)}, u32[]{:S(2)}) collective-permute-start(bf16[64,64,128]{2,1,0:T(8,128)(2,1)} %get-tuple-element.533), channel_id=1, source_target_pairs={{0,3},{1,2},{2,1},{3,0},{4,7},{5,6},{6,5},{7,4}} | collective-permute-start | bytes 3145736 | tf_op jit(solution)/shard_map/ppermute | solution.py:242
  683.8 64.8 %collective-permute-start.81 = (bf16[64,64,128]{2,1,0:T(8,128)(2,1)}, bf16[64,64,128]{2,1,0:T(8,128)(2,1)}, u32[]{:S(2)}, u32[]{:S(2)}) collective-permute-start(bf16[64,64,128]{2,1,0:T(8,128)(2,1)} %get-tuple-element.540), channel_id=1, source_target_pairs={{0,1},{1,0},{2,3},{3,2},{4,5},{5,4},{6,7},{7,6}} | collective-permute-start | bytes 3145736 | tf_op jit(solution)/shard_map/ppermute | solution.py:242
  707.5 44.9 %collective-permute-start.82 = (bf16[64,64,128]{2,1,0:T(8,128)(2,1)}, bf16[64,64,128]{2,1,0:T(8,128)(2,1)}, u32[]{:S(2)}, u32[]{:S(2)}) collective-permute-start(bf16[64,64,128]{2,1,0:T(8,128)(2,1)} %get-tuple-element.541), channel_id=1, source_target_pairs={{0,2},{1,3},{2,0},{3,1},{4,6},{5,7},{6,4},{7,5}} | collective-permute-start | bytes 3145736 | tf_op jit(solution)/shard_map/ppermute | solution.py:242
  709.1 64.9 %collective-permute-start.83 = (bf16[64,64,128]{2,1,0:T(8,128)(2,1)}, bf16[64,64,128]{2,1,0:T(8,128)(2,1)}, u32[]{:S(2)}, u32[]{:S(2)}) collective-permute-start(bf16[64,64,128]{2,1,0:T(8,128)(2,1)} %get-tuple-element.542), channel_id=1, source_target_pairs={{0,3},{1,2},{2,1},{3,0},{4,7},{5,6},{6,5},{7,4}} | collective-permute-start | bytes 3145736 | tf_op jit(solution)/shard_map/ppermute | solution.py:242
  735.9 99.6 %collective-permute-start.87 = (bf16[64,128,128]{2,1,0:T(8,128)(2,1)}, bf16[64,128,128]{2,1,0:T(8,128)(2,1)}, u32[]{:S(2)}, u32[]{:S(2)}) collective-permute-start(bf16[64,128,128]{2,1,0:T(8,128)(2,1)} %get-tuple-element.551), channel_id=1, source_target_pairs={{0,4},{4,0},{1,5},{5,1},{2,6},{6,2},{3,7},{7,3}} | collective-permute-start | bytes 6291464 | tf_op jit(solution)/shard_map/ppermute | solution.py:247
  748.0 99.6 %collective-permute-start.88 = (bf16[64,128,128]{2,1,0:T(8,128)(2,1)}, bf16[64,128,128]{2,1,0:T(8,128)(2,1)}, u32[]{:S(2)}, u32[]{:S(2)}) collective-permute-start(bf16[64,128,128]{2,1,0:T(8,128)(2,1)} %get-tuple-element.554), channel_id=1, source_target_pairs={{0,4},{4,0},{1,5},{5,1},{2,6},{6,2},{3,7},{7,3}} | collective-permute-start | bytes 6291464 | tf_op jit(solution)/shard_map/ppermute | solution.py:247
  752.4 44.9 %collective-permute-start.85 = (bf16[64,64,128]{2,1,0:T(8,128)(2,1)}, bf16[64,64,128]{2,1,0:T(8,128)(2,1)}, u32[]{:S(2)}, u32[]{:S(2)}) collective-permute-start(bf16[64,64,128]{2,1,0:T(8,128)(2,1)} %get-tuple-element.547), channel_id=1, source_target_pairs={{0,2},{1,3},{2,0},{3,1},{4,6},{5,7},{6,4},{7,5}} | collective-permute-start | bytes 3145736 | tf_op jit(solution)/shard_map/ppermute | solution.py:242
  774.0 44.9 %collective-permute-start.86 = (bf16[64,64,128]{2,1,0:T(8,128)(2,1)}, bf16[64,64,128]{2,1,0:T(8,128)(2,1)}, u32[]{:S(2)}, u32[]{:S(2)}) collective-permute-start(bf16[64,64,128]{2,1,0:T(8,128)(2,1)} %get-tuple-element.548), channel_id=1, source_target_pairs={{0,3},{1,2},{2,1},{3,0},{4,7},{5,6},{6,5},{7,4}} | collective-permute-start | bytes 3145736 | tf_op jit(solution)/shard_map/ppermute | solution.py:242
  783.0 71.4 %collective-permute-start.89 = (bf16[64,64,128]{2,1,0:T(8,128)(2,1)}, bf16[64,64,128]{2,1,0:T(8,128)(2,1)}, u32[]{:S(2)}, u32[]{:S(2)}) collective-permute-start(bf16[64,64,128]{2,1,0:T(8,128)(2,1)} %get-tuple-element.558), channel_id=1, source_target_pairs={{0,1},{1,0},{2,3},{3,2},{4,5},{5,4},{6,7},{7,6}} | collective-permute-start | bytes 3145736 | tf_op jit(solution)/shard_map/ppermute | solution.py:242
  797.4 57.7 %collective-permute-start.90 = (bf16[64,64,128]{2,1,0:T(8,128)(2,1)}, bf16[64,64,128]{2,1,0:T(8,128)(2,1)}, u32[]{:S(2)}, u32[]{:S(2)}) collective-permute-start(bf16[64,64,128]{2,1,0:T(8,128)(2,1)} %get-tuple-element.559), channel_id=1, source_target_pairs={{0,2},{1,3},{2,0},{3,1},{4,6},{5,7},{6,4},{7,5}} | collective-permute-start | bytes 3145736 | tf_op jit(solution)/shard_map/ppermute | solution.py:242
  819.0 44.9 %collective-permute-start.91 = (bf16[64,64,128]{2,1,0:T(8,128)(2,1)}, bf16[64,64,128]{2,1,0:T(8,128)(2,1)}, u32[]{:S(2)}, u32[]{:S(2)}) collective-permute-start(bf16[64,64,128]{2,1,0:T(8,128)(2,1)} %get-tuple-element.560), channel_id=1, source_target_pairs={{0,3},{1,2},{2,1},{3,0},{4,7},{5,6},{6,5},{7,4}} | collective-permute-start | bytes 3145736 | tf_op jit(solution)/shard_map/ppermute | solution.py:242
  835.5 81.3 %collective-permute-start.95 = (bf16[64,128,128]{2,1,0:T(8,128)(2,1)}, bf16[64,128,128]{2,1,0:T(8,128)(2,1)}, u32[]{:S(2)}, u32[]{:S(2)}) collective-permute-start(bf16[64,128,128]{2,1,0:T(8,128)(2,1)} %get-tuple-element.569), channel_id=1, source_target_pairs={{0,4},{4,0},{1,5},{5,1},{2,6},{6,2},{3,7},{7,3}} | collective-permute-start | bytes 6291464 | tf_op jit(solution)/shard_map/ppermute | solution.py:247
  855.0 52.9 %collective-permute-start.94 = (bf16[64,64,128]{2,1,0:T(8,128)(2,1)}, bf16[64,64,128]{2,1,0:T(8,128)(2,1)}, u32[]{:S(2)}, u32[]{:S(2)}) collective-permute-start(bf16[64,64,128]{2,1,0:T(8,128)(2,1)} %get-tuple-element.565), channel_id=1, source_target_pairs={{0,3},{1,2},{2,1},{3,0},{4,7},{5,6},{6,5},{7,4}} | collective-permute-start | bytes 3145736 | tf_op jit(solution)/shard_map/ppermute | solution.py:242
  863.9 71.8 %collective-permute-start.96 = (bf16[64,128,128]{2,1,0:T(8,128)(2,1)}, bf16[64,128,128]{2,1,0:T(8,128)(2,1)}, u32[]{:S(2)}, u32[]{:S(2)}) collective-permute-start(bf16[64,128,128]{2,1,0:T(8,128)(2,1)} %get-tuple-element.572), channel_id=1, source_target_pairs={{0,4},{4,0},{1,5},{5,1},{2,6},{6,2},{3,7},{7,3}} | collective-permute-start | bytes 6291464 | tf_op jit(solution)/shard_map/ppermute | solution.py:247
  879.1 95.1 %collective-permute-start.100 = (bf16[64,128,128]{2,1,0:T(8,128)(2,1)}, bf16[64,128,128]{2,1,0:T(8,128)(2,1)}, u32[]{:S(2)}, u32[]{:S(2)}) collective-permute-start(bf16[64,128,128]{2,1,0:T(8,128)(2,1)} %get-tuple-element.580), channel_id=1, source_target_pairs={{0,4},{4,0},{1,5},{5,1},{2,6},{6,2},{3,7},{7,3}} | collective-permute-start | bytes 6291464 | tf_op jit(solution)/shard_map/ppermute | solution.py:247
  887.2 41.0 %collective-permute-start.102 = (bf16[64,64,128]{2,1,0:T(8,128)(2,1)}, bf16[64,64,128]{2,1,0:T(8,128)(2,1)}, u32[]{:S(2)}, u32[]{:S(2)}) collective-permute-start(bf16[64,64,128]{2,1,0:T(8,128)(2,1)} %get-tuple-element.586), channel_id=1, source_target_pairs={{0,1},{1,0},{2,3},{3,2},{4,5},{5,4},{6,7},{7,6}} | collective-permute-start | bytes 3145736 | tf_op jit(solution)/shard_map/ppermute | solution.py:242
  928.3 99.7 %collective-permute-start.101 = (bf16[64,128,128]{2,1,0:T(8,128)(2,1)}, bf16[64,128,128]{2,1,0:T(8,128)(2,1)}, u32[]{:S(2)}, u32[]{:S(2)}) collective-permute-start(bf16[64,128,128]{2,1,0:T(8,128)(2,1)} %get-tuple-element.583), channel_id=1, source_target_pairs={{0,4},{4,0},{1,5},{5,1},{2,6},{6,2},{3,7},{7,3}} | collective-permute-start | bytes 6291464 | tf_op jit(solution)/shard_map/ppermute | solution.py:247
  935.7 53.4 %collective-permute-start.104 = (bf16[64,64,128]{2,1,0:T(8,128)(2,1)}, bf16[64,64,128]{2,1,0:T(8,128)(2,1)}, u32[]{:S(2)}, u32[]{:S(2)}) collective-permute-start(bf16[64,64,128]{2,1,0:T(8,128)(2,1)} %get-tuple-element.588), channel_id=1, source_target_pairs={{0,3},{1,2},{2,1},{3,0},{4,7},{5,6},{6,5},{7,4}} | collective-permute-start | bytes 3145736 | tf_op jit(solution)/shard_map/ppermute | solution.py:242
  949.3 41.2 %collective-permute-start.105 = (bf16[64,64,128]{2,1,0:T(8,128)(2,1)}, bf16[64,64,128]{2,1,0:T(8,128)(2,1)}, u32[]{:S(2)}, u32[]{:S(2)}) collective-permute-start(bf16[64,64,128]{2,1,0:T(8,128)(2,1)} %get-tuple-element.592), channel_id=1, source_target_pairs={{0,1},{1,0},{2,3},{3,2},{4,5},{5,4},{6,7},{7,6}} | collective-permute-start | bytes 3145736 | tf_op jit(solution)/shard_map/ppermute | solution.py:242
  959.5 46.0 %collective-permute-start.106 = (bf16[64,64,128]{2,1,0:T(8,128)(2,1)}, bf16[64,64,128]{2,1,0:T(8,128)(2,1)}, u32[]{:S(2)}, u32[]{:S(2)}) collective-permute-start(bf16[64,64,128]{2,1,0:T(8,128)(2,1)} %get-tuple-element.593), channel_id=1, source_target_pairs={{0,2},{1,3},{2,0},{3,1},{4,6},{5,7},{6,4},{7,5}} | collective-permute-start | bytes 3145736 | tf_op jit(solution)/shard_map/ppermute | solution.py:242
  974.3 52.0 %collective-permute-start.107 = (bf16[64,64,128]{2,1,0:T(8,128)(2,1)}, bf16[64,64,128]{2,1,0:T(8,128)(2,1)}, u32[]{:S(2)}, u32[]{:S(2)}) collective-permute-start(bf16[64,64,128]{2,1,0:T(8,128)(2,1)} %get-tuple-element.594), channel_id=1, source_target_pairs={{0,3},{1,2},{2,1},{3,0},{4,7},{5,6},{6,5},{7,4}} | collective-permute-start | bytes 3145736 | tf_op jit(solution)/shard_map/ppermute | solution.py:242
  989.1 131.5 %collective-permute-start.115 = (bf16[64,128,128]{2,1,0:T(8,128)(2,1)}, bf16[64,128,128]{2,1,0:T(8,128)(2,1)}, u32[]{:S(2)}, u32[]{:S(2)}) collective-permute-start(bf16[64,128,128]{2,1,0:T(8,128)(2,1)} %get-tuple-element.612), channel_id=1, source_target_pairs={{0,4},{4,0},{1,5},{5,1},{2,6},{6,2},{3,7},{7,3}} | collective-permute-start | bytes 6291464 | tf_op jit(solution)/shard_map/ppermute | solution.py:247
  990.6 93.9 %collective-permute-start.108 = (bf16[32,128,128]{2,1,0:T(8,128)(2,1)}, bf16[32,128,128]{2,1,0:T(8,128)(2,1)}, u32[]{:S(2)}, u32[]{:S(2)}) collective-permute-start(bf16[32,128,128]{2,1,0:T(8,128)(2,1)} %get-tuple-element.599), channel_id=1, source_target_pairs={{0,4},{4,0},{1,5},{5,1},{2,6},{6,2},{3,7},{7,3}} | collective-permute-start | bytes 3145736 | tf_op jit(solution)/shard_map/ppermute | solution.py:247
  1005.5 51.8 %collective-permute-start.109 = (bf16[32,64,128]{2,1,0:T(8,128)(2,1)}, bf16[32,64,128]{2,1,0:T(8,128)(2,1)}, u32[]{:S(2)}, u32[]{:S(2)}) collective-permute-start(bf16[32,64,128]{2,1,0:T(8,128)(2,1)} %get-tuple-element.602), channel_id=1, source_target_pairs={{0,1},{1,0},{2,3},{3,2},{4,5},{5,4},{6,7},{7,6}} | collective-permute-start | bytes 1572872 | tf_op jit(solution)/shard_map/ppermute | solution.py:242
  1107.6 50.2 %collective-permute-start.118 = (bf16[64,64,128]{2,1,0:T(8,128)(2,1)}, bf16[64,64,128]{2,1,0:T(8,128)(2,1)}, u32[]{:S(2)}, u32[]{:S(2)}) collective-permute-start(bf16[64,64,128]{2,1,0:T(8,128)(2,1)} %get-tuple-element.617), channel_id=1, source_target_pairs={{0,3},{1,2},{2,1},{3,0},{4,7},{5,6},{6,5},{7,4}} | collective-permute-start | bytes 3145736 | tf_op jit(solution)/shard_map/ppermute | solution.py:242
  1119.1 47.3 %collective-permute-start.122 = (bf16[32,128,128]{2,1,0:T(8,128)(2,1)}, bf16[32,128,128]{2,1,0:T(8,128)(2,1)}, u32[]{:S(2)}, u32[]{:S(2)}) collective-permute-start(bf16[32,128,128]{2,1,0:T(8,128)(2,1)} %get-tuple-element.626), channel_id=1, source_target_pairs={{0,4},{4,0},{1,5},{5,1},{2,6},{6,2},{3,7},{7,3}} | collective-permute-start | bytes 3145736 | tf_op jit(solution)/shard_map/ppermute | solution.py:247
  1120.6 57.5 %collective-permute-start.123 = (bf16[32,128,128]{2,1,0:T(8,128)(2,1)}, bf16[32,128,128]{2,1,0:T(8,128)(2,1)}, u32[]{:S(2)}, u32[]{:S(2)}) collective-permute-start(bf16[32,128,128]{2,1,0:T(8,128)(2,1)} %get-tuple-element.629), channel_id=1, source_target_pairs={{0,4},{4,0},{1,5},{5,1},{2,6},{6,2},{3,7},{7,3}} | collective-permute-start | bytes 3145736 | tf_op jit(solution)/shard_map/ppermute | solution.py:247
  1124.3 52.2 %collective-permute-start.129 = (bf16[16,64,128]{2,1,0:T(8,128)(2,1)}, bf16[16,64,128]{2,1,0:T(8,128)(2,1)}, u32[]{:S(2)}, u32[]{:S(2)}) collective-permute-start(bf16[16,64,128]{2,1,0:T(8,128)(2,1)} %get-tuple-element.644), channel_id=1, source_target_pairs={{0,1},{1,0},{2,3},{3,2},{4,5},{5,4},{6,7},{7,6}} | collective-permute-start | bytes 786440 | tf_op jit(solution)/shard_map/ppermute | solution.py:242
  1135.7 78.5 %collective-permute-start.124 = (bf16[64,64,128]{2,1,0:T(8,128)(2,1)}, bf16[64,64,128]{2,1,0:T(8,128)(2,1)}, u32[]{:S(2)}, u32[]{:S(2)}) collective-permute-start(bf16[64,64,128]{2,1,0:T(8,128)(2,1)} %get-tuple-element.632), channel_id=1, source_target_pairs={{0,1},{1,0},{2,3},{3,2},{4,5},{5,4},{6,7},{7,6}} | collective-permute-start | bytes 3145736 | tf_op jit(solution)/shard_map/ppermute | solution.py:242
  1157.8 56.8 %collective-permute-start.125 = (bf16[64,64,128]{2,1,0:T(8,128)(2,1)}, bf16[64,64,128]{2,1,0:T(8,128)(2,1)}, u32[]{:S(2)}, u32[]{:S(2)}) collective-permute-start(bf16[64,64,128]{2,1,0:T(8,128)(2,1)} %get-tuple-element.633), channel_id=1, source_target_pairs={{0,2},{1,3},{2,0},{3,1},{4,6},{5,7},{6,4},{7,5}} | collective-permute-start | bytes 3145736 | tf_op jit(solution)/shard_map/ppermute | solution.py:242
  1166.4 54.2 %collective-permute-start.126 = (bf16[64,64,128]{2,1,0:T(8,128)(2,1)}, bf16[64,64,128]{2,1,0:T(8,128)(2,1)}, u32[]{:S(2)}, u32[]{:S(2)}) collective-permute-start(bf16[64,64,128]{2,1,0:T(8,128)(2,1)} %get-tuple-element.634), channel_id=1, source_target_pairs={{0,3},{1,2},{2,1},{3,0},{4,7},{5,6},{6,5},{7,4}} | collective-permute-start | bytes 3145736 | tf_op jit(solution)/shard_map/ppermute | solution.py:242
  1176.5 52.3 %collective-permute-start.128 = (bf16[32,128,128]{2,1,0:T(8,128)(2,1)}, bf16[32,128,128]{2,1,0:T(8,128)(2,1)}, u32[]{:S(2)}, u32[]{:S(2)}) collective-permute-start(bf16[32,128,128]{2,1,0:T(8,128)(2,1)} %get-tuple-element.641), channel_id=1, source_target_pairs={{0,4},{4,0},{1,5},{5,1},{2,6},{6,2},{3,7},{7,3}} | collective-permute-start | bytes 3145736 | tf_op jit(solution)/shard_map/ppermute | solution.py:247
  (104 other events, 2169.7 us)
